TPU v7x, 1024 devices: a whole 4x4x32 slice. The times are simulated.
1024 devices in a mesh: blk: 16 (over z_hi, x, core), group: 64 (over y, z_lo).
Axes of the slice: x: 4, y: 4, z: 32 (z_hi: 2, z_lo: 16; z = z_hi * 16 + z_lo), core: 2. Of those that a mesh axis runs over, the one named last changes fastest.
Arguments:
- queries: bfloat16 [64, 2048, 2048], P('group', 'blk'), may hold values from -300 to 300
- normed: bfloat16 [64, 2048, 2048], P('group', 'blk'), may hold values from -6 to 6
- key_weight_copies: bfloat16 [64, 2048, 512], P('group', 'blk'), may hold values from -0.125 to 0.125
- value_weight_copies: bfloat16 [64, 2048, 512], P('group', 'blk'), may hold values from -0.125 to 0.125
- owner: int32 [16], replicated, may hold values from 0 to 63
Outputs:
- cache_keys: bfloat16 [64, 2048, 512], P('group', 'blk')
- cache_values: bfloat16 [64, 2048, 512], P('group', 'blk')
- attended: bfloat16 [64, 2048, 2048], P('group', 'blk')
Inputs may be any that keep to these rules, and one draw needn't show every extreme that they name: `owner`: learner group index of each block of projection rows, below the number of actor groups.
All inputs are finite; a program needn't handle non-finite values.
Results may differ from a plain program's by a relative error of at most 0.011.
Values may be sent and summed in bfloat16 or wider, within the bound.
No kernel may reach another device: no remote copies, remote signals or barrier semaphores. Data moves between devices by JAX's collectives and lax.ppermute only.
A program may use at most 64 MiB of HBM per device.

v0:
```python
import math

import jax
import jax.numpy as jnp
from jax import lax
from jax.experimental import pallas as pl
from jax.experimental.pallas import tpu as pltpu
from jax.sharding import Mesh
from jax.sharding import PartitionSpec as P


HEAD = 128
SCALE = HEAD ** (-0.5)
NEG = -1e30
QB = 256
CHUNKS = 2
STEP = 1024 // CHUNKS
AXES = ("zh", "x", "c", "y", "zf", "zn")
RING = ("zh", "zf", "zn")
VM = pl.BlockSpec(memory_space=pltpu.VMEM)
SM = pl.BlockSpec(memory_space=pltpu.SMEM)
NT = (((1,), (1,)), ((), ()))
STATE = (
    jax.ShapeDtypeStruct((1024, 256), jnp.float32),
    jax.ShapeDtypeStruct((1024, 4), jnp.float32),
)


def exchange(x, axes):
    return lax.all_to_all(x, axes, 0, 0, tiled=True)


def spread(x, axes, n):
    return exchange(jnp.broadcast_to(x[None], (n,) + x.shape), axes)


def pick(x, index):
    n = index.shape[0]

    def kernel(i_ref, x_ref, o_ref):
        for k in range(n):
            o_ref[k] = x_ref[i_ref[k]]

    return pl.pallas_call(
        kernel,
        out_shape=jax.ShapeDtypeStruct((n,) + x.shape[1:], x.dtype),
        in_specs=[SM, VM],
        out_specs=VM,
        name="pick",
    )(index, x)


def tables(zh, c):
    half = HEAD // 2
    freq = jnp.exp(
        jnp.arange(half).astype(jnp.float32) * (-2.0 * math.log(500000.0) / HEAD)
    )
    t = zh * 1024 + jnp.arange(1024, dtype=jnp.int32)
    angles = t.astype(jnp.float32)[:, None] * freq[None, :]
    cos, sin = jnp.cos(angles), jnp.sin(angles)
    cos = jnp.concatenate([cos, cos], axis=1)
    sin = jnp.concatenate([-sin, sin], axis=1)
    is_key = c == 0
    return jnp.where(is_key, cos, 1.0), jnp.where(is_key, sin, 0.0)


def project(place, mine, other, w, cos, sin):
    def kernel(p_ref, a0, a1, a2, a3, b_ref, w_ref, cos_ref, sin_ref, o_ref):
        for k in range(8):
            s = k % 4
            piece = (a0, a1, a2, a3)[s][...] if k < 4 else b_ref[s]
            raw = jnp.dot(piece, w_ref[...], preferred_element_type=jnp.float32)
            rows = pl.ds(pl.multiple_of(p_ref[k] * 128, 128), 128)
            turned = raw * cos_ref[rows, :] + pltpu.roll(raw, 64, 1) * sin_ref[rows, :]
            o_ref[rows, :] = turned.astype(jnp.bfloat16)

    return pl.pallas_call(
        kernel,
        out_shape=jax.ShapeDtypeStruct((1024, HEAD), jnp.bfloat16),
        in_specs=[SM] + [VM] * 8,
        out_specs=VM,
        name="project",
    )(place, *mine, other, w, cos, sin)


def attend_own(q, k, v):
    def kernel(q_ref, k_ref, v_ref, acc_ref, st_ref):
        for i in range(1024 // QB):
            rows = pl.ds(i * QB, QB)
            n = (i + 1) * QB
            r = lax.broadcasted_iota(jnp.int32, (QB, n), 0) + i * QB
            t = lax.broadcasted_iota(jnp.int32, (QB, n), 1)
            tops, totals = [], []
            for h in range(2):
                col = pl.ds(h * HEAD, HEAD)
                s = lax.dot_general(
                    q_ref[rows, col], k_ref[:n, :], NT, preferred_element_type=jnp.float32
                )
                s = jnp.where(t <= r, s, NEG)
                m = jnp.max(s, axis=1, keepdims=True)
                p = jnp.exp((s - m) * SCALE)
                tops.append(m)
                totals.append(jnp.sum(p, axis=1, keepdims=True))
                acc_ref[rows, col] = jnp.dot(
                    p.astype(jnp.bfloat16), v_ref[:n, :], preferred_element_type=jnp.float32
                )
            st_ref[rows, :] = jnp.concatenate(tops + totals, axis=1)

    return pl.pallas_call(
        kernel,
        out_shape=STATE,
        in_specs=[VM] * 3,
        out_specs=(VM,) * 2,
        name="attend_own",
    )(q, k, v)


def attend_more(zh, q, k, v, acc, st, last):
    n = k.shape[0]

    def kernel(z_ref, q_ref, k_ref, v_ref, acc_ref, st_ref, *outs):
        def leave(col, acc, total):
            if last:
                outs[0][:, col] = (acc / total).astype(jnp.bfloat16)
            else:
                outs[0][:, col] = acc

        @pl.when(z_ref[0] == 0)
        def _():
            for h in range(2):
                col = pl.ds(h * HEAD, HEAD)
                leave(col, acc_ref[:, col], st_ref[:, 2 + h : 3 + h])
            if not last:
                outs[1][...] = st_ref[...]

        @pl.when(z_ref[0] != 0)
        def _():
            tops, totals = [], []
            for h in range(2):
                col = pl.ds(h * HEAD, HEAD)
                s = lax.dot_general(
                    q_ref[:, col], k_ref[...], NT, preferred_element_type=jnp.float32
                )
                m0 = st_ref[:, h : h + 1]
                m1 = jnp.maximum(m0, jnp.max(s, axis=1, keepdims=True))
                fade = jnp.exp((m0 - m1) * SCALE)
                p = jnp.exp((s - m1) * SCALE)
                total = st_ref[:, 2 + h : 3 + h] * fade + jnp.sum(p, axis=1, keepdims=True)
                out = acc_ref[:, col] * fade + jnp.dot(
                    p.astype(jnp.bfloat16), v_ref[...], preferred_element_type=jnp.float32
                )
                leave(col, out, total)
                tops.append(m1)
                totals.append(total)
            if not last:
                outs[1][...] = jnp.concatenate(tops + totals, axis=1)

    row = lambda width: pl.BlockSpec((QB, width), lambda i: (i, 0))
    whole = pl.BlockSpec((n, HEAD), lambda i: (0, 0))
    out = jax.ShapeDtypeStruct((1024, 256), jnp.bfloat16)
    return pl.pallas_call(
        kernel,
        grid=(1024 // QB,),
        out_shape=out if last else STATE,
        in_specs=[SM, row(256), whole, whole, row(256), row(4)],
        out_specs=row(256) if last else (row(256), row(4)),
        name="attend_more",
    )(zh.reshape(1), q, k, v, acc, st)


def swap_cores(x):
    return lax.ppermute(x, "c", [(0, 1), (1, 0)])


def layer(queries, normed, key_weight_copies, value_weight_copies, owner):
    zh, x, c = lax.axis_index("zh"), lax.axis_index("x"), lax.axis_index("c")
    z_lo = lax.axis_index(("zf", "zn"))
    own_y, own_zf, own_zn = owner // 16, (owner // 4) % 4, owner % 4
    block8 = jnp.arange(8, dtype=jnp.int32)
    n = normed[0]

    w = jnp.stack([key_weight_copies[0], value_weight_copies[0]])
    w = w.reshape(2, 16, 8, 4, HEAD).transpose(3, 0, 1, 2, 4).reshape(128, 8, HEAD)
    w = exchange(w, ("x", "c", "y", "zn"))
    here = lax.dynamic_slice_in_dim(own_y * 4 + own_zn, zh * 8, 8)
    w = pick(w, block8 * 16 + here)

    rows = [n]
    for s in (1, 2, 3):
        rows.append(lax.ppermute(n, "x", [(i, (i + s) % 4) for i in range(4)]))

    w = spread(w, ("zh", "zf"), 8)
    block16 = jnp.arange(16, dtype=jnp.int32)
    w = pick(w.reshape(64, 8, HEAD), ((block16 // 8) * 4 + own_zf) * 8 + block16 % 8)

    other = swap_cores(jnp.stack(rows))

    w = spread(w, ("y", "zn"), 16).reshape(16, 16, 8, HEAD)
    w = w.transpose(1, 0, 2, 3).reshape(2048, HEAD)

    chip = (x - jnp.arange(4, dtype=jnp.int32)) % 4
    place = jnp.concatenate([chip * 2 + c, chip * 2 + 1 - c])
    cos, sin = tables(zh, c)
    kv = project(place, rows, other, w, cos, sin)

    ups, downs = [], []
    for k in range(CHUNKS):
        part = kv[k * STEP : (k + 1) * STEP]
        ups.append(lax.ppermute(part, RING, [(i, i + 15) for i in range(8, 16)]))
        downs.append(lax.ppermute(part, RING, [(i, i + 17) for i in range(8)]))

    partner = swap_cores(kv)
    keys, values = jnp.where(c == 0, kv, partner), jnp.where(c == 0, partner, kv)
    q = queries[0].reshape(128, 8, 256).transpose(1, 0, 2)
    q = exchange(q, ("x", "c")).reshape(1024, 256)
    state = attend_own(q, keys, values)
    cache = exchange(kv.reshape(8, 128, HEAD), ("x", "c")).reshape(4, 2, 128, HEAD)
    cache_keys = cache[:, 0].transpose(1, 0, 2).reshape(1, 128, 512)
    cache_values = cache[:, 1].transpose(1, 0, 2).reshape(1, 128, 512)

    ups[0], downs[0], state, cache_keys, cache_values = lax.optimization_barrier(
        (ups[0], downs[0], state, cache_keys, cache_values)
    )
    for k in range(CHUNKS):
        if k:
            ups[k], downs[k], state = lax.optimization_barrier((ups[k], downs[k], state))
        up = lax.ppermute(ups[k], RING, [(i, i + 1) for i in range(23, 31)])
        down = lax.ppermute(downs[k], RING, [(i, i - 1) for i in range(17, 25)])
        first = jnp.where(z_lo >= 8, up, down)
        partner = swap_cores(first)
        keys, values = jnp.where(c == 0, first, partner), jnp.where(c == 0, partner, first)
        state = attend_more(zh, q, keys, values, *state, k == CHUNKS - 1)
    out = exchange(state.reshape(8, 128, 256), ("x", "c"))
    attended = out.transpose(1, 0, 2).reshape(1, 128, 2048)
    return cache_keys, cache_values, attended


def solution(mesh):
    torus = Mesh(mesh.devices.reshape(2, 4, 2, 4, 4, 4), AXES)
    spec = P(("y", "zf", "zn"), ("zh", "x", "c"), None)
    return jax.shard_map(
        layer,
        mesh=torus,
        in_specs=(spec, spec, spec, spec, P()),
        out_specs=(spec, spec, spec),
        check_vma=False,
    )
```

profile of v0, /device:TPU:960, one launch (start us, length us, event | category | flops | bytes accessed | tf_op | source)
XLA Modules:
  0.0 257.2 jit_solution(13058791140036034639)
XLA Ops:
  2.4 11.1 %all-to-all-start = ((bf16[128,8,128]{2,1,0:T(8,128)(2,1)}), bf16[128,8,128]{2,1,0:T(8,128)(2,1)S(1)}, u32[]{:S(2)}, u32[]{:S(2)}) async-start(bf16[128,8,128]{2,1,0:T(8,128)(2,1)} %bitcast.6), calls=%async_computation | async-start | bytes 524288 | tf_op jit(solution)/shard_map/all_to_all | solution.py:30
  15.3 9.6 %all-to-all-done.x_ref = bf16[128,8,128]{2,1,0:T(8,128)(2,1)S(1)} async-done(((bf16[128,8,128]{2,1,0:T(8,128)(2,1)}), bf16[128,8,128]{2,1,0:T(8,128)(2,1)S(1)}, u32[]{:S(2)}, u32[]{:S(2)}) %all-to-all-start) | async-done | bytes 262176 | tf_op jit(solution)/shard_map/all_to_all | solution.py:30
  28.0 42.9 %all_to_all.30 = bf16[8,8,8,128]{3,2,1,0:T(8,128)(2,1)} all-to-all(bf16[8,8,8,128]{3,2,1,0:T(8,128)(2,1)S(1)} %broadcast_in_dim.10), channel_id=1, replica_groups=mesh['zh'=2,'x'=4,'c'=2,'y'=4,'zf'=4,'zn'=4] {'zh','zf'}, dimensions={0} | all-to-all | bytes 262144 | tf_op jit(solution)/shard_map/all_to_all | solution.py:30
  74.1 4.6 %all-to-all-start.2 = ((bf16[16,16,8,128]{3,2,1,0:T(8,128)(2,1)}), bf16[16,16,8,128]{3,2,1,0:T(8,128)(2,1)S(1)}, u32[]{:S(2)}, u32[]{:S(2)}) async-start(bf16[16,16,8,128]{3,2,1,0:T(8,128)(2,1)} %broadcast_in_dim.22), calls=%async_computation.2 | async-start | bytes 1048576 | tf_op jit(solution)/shard_map/all_to_all | solution.py:30
  78.7 2.5 collective-permute-start
  81.2 3.5 %collective-permute-start.1 = (bf16[128,2048]{1,0:T(8,128)(2,1)S(1)}, bf16[128,2048]{1,0:T(8,128)(2,1)S(1)}, u32[]{:S(2)}, u32[]{:S(2)}) collective-permute-start(bf16[128,2048]{1,0:T(8,128)(2,1)S(1)} %bitcast.45), channel_id=1, source_target_pairs={{0,256},{128,384},{256,0},{384,128},{1,257},{129,385},{257,1},{385... | collective-permute-start | bytes 1572872 | tf_op jit(solution)/shard_map/ppermute | solution.py:190
  84.7 3.5 %collective-permute-start.2 = (bf16[128,2048]{1,0:T(8,128)(2,1)S(1)}, bf16[128,2048]{1,0:T(8,128)(2,1)S(1)}, u32[]{:S(2)}, u32[]{:S(2)}) collective-permute-start(bf16[128,2048]{1,0:T(8,128)(2,1)S(1)} %bitcast.46), channel_id=1, source_target_pairs={{0,384},{128,0},{256,128},{384,256},{1,385},{129,1},{257,129},{385... | collective-permute-start | bytes 1572872 | tf_op jit(solution)/shard_map/ppermute | solution.py:190
  88.2 17.7 %collective-permute-done.a1 = bf16[128,2048]{1,0:T(8,128)(2,1)S(1)} collective-permute-done((bf16[128,2048]{1,0:T(8,128)(2,1)S(1)}, bf16[128,2048]{1,0:T(8,128)(2,1)S(1)}, u32[]{:S(2)}, u32[]{:S(2)}) %collective-permute-start) | collective-permute-done | bytes 524320 | tf_op jit(solution)/shard_map/ppermute | solution.py:190
  106.0 2.5 collective-permute-done.2.a3
  120.3 4.6 %project.1 = bf16[1024,128]{1,0:T(8,128)(2,1)} custom-call(s32[8]{0:T(128)} %pad_add_fusion.p_ref, bf16[128,2048]{1,0:T(8,128)(2,1)} %bitcast.43, bf16[128,2048]{1,0:T(8,128)(2,1)} %copy-done.4, bf16[128,2048]{1,0:T(8,128)(2,1)} %copy-done.5, bf16[128,2048]{1,0:T(8,128)(2,1)} %copy-done.6, bf16[4,128,2048]{2,1,0:T(8,128)(2,1)} %copy-done.2, ...), custom_call_target="tpu_custom_call" | custom-call | tf_op jit(solution)/shard_map/project/pallas_call | solution.py:77
  124.9 2.5 collective-permute-start.6
  127.4 3.9 %all-to-all-start.4 = ((bf16[8,128,128]{2,1,0:T(8,128)(2,1)}), bf16[8,128,128]{2,1,0:T(8,128)(2,1)S(1)}, u32[]{:S(2)}, u32[]{:S(2)}) async-start(bf16[8,128,128]{2,1,0:T(8,128)(2,1)} %bitcast.37), calls=%async_computation.4 | async-start | bytes 524288 | tf_op jit(solution)/shard_map/all_to_all | solution.py:30
  134.3 4.5 %all-to-all-done.4 = bf16[8,128,128]{2,1,0:T(8,128)(2,1)S(1)} async-done(((bf16[8,128,128]{2,1,0:T(8,128)(2,1)}), bf16[8,128,128]{2,1,0:T(8,128)(2,1)S(1)}, u32[]{:S(2)}, u32[]{:S(2)}) %all-to-all-start.4) | async-done | bytes 262176 | tf_op jit(solution)/shard_map/all_to_all | solution.py:30
  138.9 3.5 %all-to-all-start.3 = ((bf16[8,128,256]{2,1,0:T(8,128)(2,1)}), bf16[8,128,256]{2,1,0:T(8,128)(2,1)S(1)}, u32[]{:S(2)}, u32[]{:S(2)}) async-start(bf16[8,128,256]{2,1,0:T(8,128)(2,1)} %bitcast.31), calls=%async_computation.3 | async-start | bytes 1048576 | tf_op jit(solution)/shard_map/all_to_all | solution.py:30
  144.9 7.7 %all-to-all-done.3 = bf16[8,128,256]{2,1,0:T(8,128)(2,1)S(1)} async-done(((bf16[8,128,256]{2,1,0:T(8,128)(2,1)}), bf16[8,128,256]{2,1,0:T(8,128)(2,1)S(1)}, u32[]{:S(2)}, u32[]{:S(2)}) %all-to-all-start.3) | async-done | bytes 524320 | tf_op jit(solution)/shard_map/all_to_all | solution.py:30
  153.4 5.5 %attend_own.1 = (f32[1024,256]{1,0:T(8,128)}, f32[1024,4]{1,0:T(8,128)}) custom-call(bf16[1024,256]{1,0:T(8,128)(2,1)} %bitcast.34, bf16[1024,128]{1,0:T(8,128)(2,1)} %get-tuple-element.32.k_ref, bf16[1024,128]{1,0:T(8,128)(2,1)} %get-tuple-element.31.v_ref), custom_call_target="tpu_custom_call" | custom-call | tf_op jit(solution)/shard_map/attend_own/pallas_call | solution.py:109
  158.9 17.3 %collective-permute-done.4 = bf16[512,128]{1,0:T(8,128)(2,1)S(1)} collective-permute-done((bf16[512,128]{1,0:T(8,128)(2,1)S(1)}, bf16[512,128]{1,0:T(8,128)(2,1)S(1)}, u32[]{:S(2)}, u32[]{:S(2)}) %collective-permute-start.4) | collective-permute-done | bytes 131104 | tf_op jit(solution)/shard_map/ppermute | solution.py:209
  178.9 4.5 %collective-permute-done.9 = bf16[512,128]{1,0:T(8,128)(2,1)S(1)} collective-permute-done((bf16[512,128]{1,0:T(8,128)(2,1)S(1)}, bf16[512,128]{1,0:T(8,128)(2,1)S(1)}, u32[]{:S(2)}, u32[]{:S(2)}) %collective-permute-start.9) | collective-permute-done | bytes 131104 | tf_op jit(solution)/shard_map/ppermute | solution.py:227
  188.2 6.0 %attend_more.2 = (f32[1024,256]{1,0:T(8,128)}, f32[1024,4]{1,0:T(8,128)}) custom-call(s32[1]{0:T(128)} %bitcast.18.z_ref, bf16[1024,256]{1,0:T(8,128)(2,1)} %bitcast.35, bf16[512,128]{1,0:T(8,128)(2,1)} %get-tuple-element.36.k_ref, bf16[512,128]{1,0:T(8,128)(2,1)} %get-tuple-element.35.v_ref, f32[1024,256]{1,0:T(8,128)} %get-tuple-element.23.acc_ref, ...), custom_call_target="tpu_custom_call" | custom-call | tf_op jit(solution)/shard_map/attend_more/pallas_call | solution.py:161
  194.2 29.5 %collective-permute-done.7 = bf16[512,128]{1,0:T(8,128)(2,1)S(1)} collective-permute-done((bf16[512,128]{1,0:T(8,128)(2,1)S(1)}, bf16[512,128]{1,0:T(8,128)(2,1)S(1)}, u32[]{:S(2)}, u32[]{:S(2)}) %collective-permute-start.7) | collective-permute-done | bytes 131104 | tf_op jit(solution)/shard_map/ppermute | solution.py:209
  226.3 4.5 %collective-permute-done.12 = bf16[512,128]{1,0:T(8,128)(2,1)S(1)} collective-permute-done((bf16[512,128]{1,0:T(8,128)(2,1)S(1)}, bf16[512,128]{1,0:T(8,128)(2,1)S(1)}, u32[]{:S(2)}, u32[]{:S(2)}) %collective-permute-start.12) | collective-permute-done | bytes 131104 | tf_op jit(solution)/shard_map/ppermute | solution.py:227
  230.7 1.9 collective-permute-start.14
  234.7 6.4 %attend_more.3 = bf16[1024,256]{1,0:T(8,128)(2,1)} custom-call(s32[1]{0:T(128)} %bitcast.18.z_ref, bf16[1024,256]{1,0:T(8,128)(2,1)} %bitcast.36, bf16[512,128]{1,0:T(8,128)(2,1)} %get-tuple-element.34.k_ref, bf16[512,128]{1,0:T(8,128)(2,1)} %get-tuple-element.33.v_ref, f32[1024,256]{1,0:T(8,128)} %get-tuple-element.29.acc_ref, ...), custom_call_target="tpu_custom_call" | custom-call | tf_op jit(solution)/shard_map/attend_more/pallas_call | solution.py:161
  241.1 14.8 %all_to_all.31 = bf16[8,128,256]{2,1,0:T(8,128)(2,1)S(1)} all-to-all(bf16[8,128,256]{2,1,0:T(8,128)(2,1)} %bitcast.42), channel_id=1, replica_groups=mesh['zh'=2,'x'=4,'c'=2,'y'=4,'zf'=4,'zn'=4] {'x','c'}, dimensions={0} | all-to-all | bytes 1048576 | tf_op jit(solution)/shard_map/all_to_all | solution.py:30
  (67 shorter events, 41.1 us)
Async XLA Ops:
  0.6 78.0 %copy-start.3 = (bf16[1,128,2048]{2,1,0:T(8,128)(2,1)S(1)}, bf16[1,128,2048]{2,1,0:T(8,128)(2,1)}, u32[]{:S(2)}) copy-start(bf16[1,128,2048]{2,1,0:T(8,128)(2,1)} %param.6) | copy-start | bytes 1572868
  2.4 22.5 %all-to-all-start = ((bf16[128,8,128]{2,1,0:T(8,128)(2,1)}), bf16[128,8,128]{2,1,0:T(8,128)(2,1)S(1)}, u32[]{:S(2)}, u32[]{:S(2)}) async-start(bf16[128,8,128]{2,1,0:T(8,128)(2,1)} %bitcast.6), calls=%async_computation | async-start | bytes 524288 | tf_op jit(solution)/shard_map/all_to_all | solution.py:30
  74.1 43.9 %all-to-all-start.2 = ((bf16[16,16,8,128]{3,2,1,0:T(8,128)(2,1)}), bf16[16,16,8,128]{3,2,1,0:T(8,128)(2,1)S(1)}, u32[]{:S(2)}, u32[]{:S(2)}) async-start(bf16[16,16,8,128]{3,2,1,0:T(8,128)(2,1)} %broadcast_in_dim.22), calls=%async_computation.2 | async-start | bytes 1048576 | tf_op jit(solution)/shard_map/all_to_all | solution.py:30
  78.7 27.3 %collective-permute-start = (bf16[128,2048]{1,0:T(8,128)(2,1)S(1)}, bf16[128,2048]{1,0:T(8,128)(2,1)S(1)}, u32[]{:S(2)}, u32[]{:S(2)}) collective-permute-start(bf16[128,2048]{1,0:T(8,128)(2,1)S(1)} %bitcast.44), channel_id=1, source_target_pairs={{0,128},{128,256},{256,384},{384,0},{1,129},{129,257},{257,385},{3... | collective-permute-start | bytes 1572872 | tf_op jit(solution)/shard_map/ppermute | solution.py:190
  81.2 24.8 %collective-permute-start.1 = (bf16[128,2048]{1,0:T(8,128)(2,1)S(1)}, bf16[128,2048]{1,0:T(8,128)(2,1)S(1)}, u32[]{:S(2)}, u32[]{:S(2)}) collective-permute-start(bf16[128,2048]{1,0:T(8,128)(2,1)S(1)} %bitcast.45), channel_id=1, source_target_pairs={{0,256},{128,384},{256,0},{384,128},{1,257},{129,385},{257,1},{385... | collective-permute-start | bytes 1572872 | tf_op jit(solution)/shard_map/ppermute | solution.py:190
  84.7 23.7 %collective-permute-start.2 = (bf16[128,2048]{1,0:T(8,128)(2,1)S(1)}, bf16[128,2048]{1,0:T(8,128)(2,1)S(1)}, u32[]{:S(2)}, u32[]{:S(2)}) collective-permute-start(bf16[128,2048]{1,0:T(8,128)(2,1)S(1)} %bitcast.46), channel_id=1, source_target_pairs={{0,384},{128,0},{256,128},{384,256},{1,385},{129,1},{257,129},{385... | collective-permute-start | bytes 1572872 | tf_op jit(solution)/shard_map/ppermute | solution.py:190
  106.0 4.2 %copy-start.4 = (bf16[128,2048]{1,0:T(8,128)(2,1)}, bf16[128,2048]{1,0:T(8,128)(2,1)S(1)}, u32[]{:S(2)}) copy-start(bf16[128,2048]{1,0:T(8,128)(2,1)S(1)} %collective-permute-done.a1) | copy-start | bytes 1572868
  106.0 4.2 %copy-start.5 = (bf16[128,2048]{1,0:T(8,128)(2,1)}, bf16[128,2048]{1,0:T(8,128)(2,1)S(1)}, u32[]{:S(2)}) copy-start(bf16[128,2048]{1,0:T(8,128)(2,1)S(1)} %collective-permute-done.1.a2) | copy-start | bytes 1572868
  108.5 1.6 copy-start.6
  110.1 8.8 %collective-permute-start.3 = (bf16[4,128,2048]{2,1,0:T(8,128)(2,1)}, bf16[4,128,2048]{2,1,0:T(8,128)(2,1)S(1)}, u32[]{:S(2)}, u32[]{:S(2)}) collective-permute-start(bf16[4,128,2048]{2,1,0:T(8,128)(2,1)} %pad_maximum_fusion), channel_id=1, source_target_pairs={{0,64},{64,0},{1,65},{65,1},{2,66},{66,2},{3,67},{67,3},{4,68},{68... | collective-permute-start | bytes 6291464 | tf_op jit(solution)/shard_map/ppermute | solution.py:172
  124.9 19.1 %copy-start.1 = (bf16[1024,128]{1,0:T(8,128)(2,1)S(1)}, bf16[1024,128]{1,0:T(8,128)(2,1)}, u32[]{:S(2)}) copy-start(bf16[1024,128]{1,0:T(8,128)(2,1)} %project.1) | copy-start | bytes 786436
  124.9 19.1 %collective-permute-start.6 = (bf16[1024,128]{1,0:T(8,128)(2,1)}, bf16[1024,128]{1,0:T(8,128)(2,1)S(1)}, u32[]{:S(2)}, u32[]{:S(2)}) collective-permute-start(bf16[1024,128]{1,0:T(8,128)(2,1)} %project.1), channel_id=1, source_target_pairs={{0,64},{64,0},{1,65},{65,1},{2,66},{66,2},{3,67},{67,3},{4,68},{68... | collective-permute-start | bytes 786440 | tf_op jit(solution)/shard_map/ppermute | solution.py:172
  127.4 11.4 %all-to-all-start.4 = ((bf16[8,128,128]{2,1,0:T(8,128)(2,1)}), bf16[8,128,128]{2,1,0:T(8,128)(2,1)S(1)}, u32[]{:S(2)}, u32[]{:S(2)}) async-start(bf16[8,128,128]{2,1,0:T(8,128)(2,1)} %bitcast.37), calls=%async_computation.4 | async-start | bytes 524288 | tf_op jit(solution)/shard_map/all_to_all | solution.py:30
  132.4 43.9 %collective-permute-start.4 = (bf16[512,128]{1,0:T(8,128)(2,1)S(1)}, bf16[512,128]{1,0:T(8,128)(2,1)S(1)}, u32[]{:S(2)}, u32[]{:S(2)}) collective-permute-start(bf16[512,128]{1,0:T(8,128)(2,1)S(1)} %get-tuple-element.38), channel_id=1, source_target_pairs={{8,519},{9,520},{10,521},{11,522},{12,523},{13,524},{14,525},{15,5... | collective-permute-start | bytes 393224 | tf_op jit(solution)/shard_map/ppermute | solution.py:209
  133.7 42.6 %collective-permute-start.5 = (bf16[512,128]{1,0:T(8,128)(2,1)S(1)}, bf16[512,128]{1,0:T(8,128)(2,1)S(1)}, u32[]{:S(2)}, u32[]{:S(2)}) collective-permute-start(bf16[512,128]{1,0:T(8,128)(2,1)S(1)} %get-tuple-element.38), channel_id=1, source_target_pairs={{0,513},{1,514},{2,515},{3,516},{4,517},{5,518},{6,519},{7,520},{1... | collective-permute-start | bytes 393224 | tf_op jit(solution)/shard_map/ppermute | solution.py:210
  138.9 13.7 %all-to-all-start.3 = ((bf16[8,128,256]{2,1,0:T(8,128)(2,1)}), bf16[8,128,256]{2,1,0:T(8,128)(2,1)S(1)}, u32[]{:S(2)}, u32[]{:S(2)}) async-start(bf16[8,128,256]{2,1,0:T(8,128)(2,1)} %bitcast.31), calls=%async_computation.3 | async-start | bytes 1048576 | tf_op jit(solution)/shard_map/all_to_all | solution.py:30
  176.3 7.1 %collective-permute-start.9 = (bf16[512,128]{1,0:T(8,128)(2,1)S(1)}, bf16[512,128]{1,0:T(8,128)(2,1)S(1)}, u32[]{:S(2)}, u32[]{:S(2)}) collective-permute-start(bf16[512,128]{1,0:T(8,128)(2,1)S(1)} %collective-permute-done.4), channel_id=1, source_target_pairs={{519,520},{520,521},{521,522},{522,523},{523,524},{524,525},{525,5... | collective-permute-start | bytes 393224 | tf_op jit(solution)/shard_map/ppermute | solution.py:227
  178.2 5.1 %collective-permute-start.10 = (bf16[512,128]{1,0:T(8,128)(2,1)S(1)}, bf16[512,128]{1,0:T(8,128)(2,1)S(1)}, u32[]{:S(2)}, u32[]{:S(2)}) collective-permute-start(bf16[512,128]{1,0:T(8,128)(2,1)S(1)} %collective-permute-done.5), channel_id=1, source_target_pairs={{513,512},{514,513},{515,514},{516,515},{517,516},{518,517},{519,5... | collective-permute-start | bytes 393224 | tf_op jit(solution)/shard_map/ppermute | solution.py:228
  183.3 4.1 %collective-permute-start.11 = (bf16[512,128]{1,0:T(8,128)(2,1)S(1)}, bf16[512,128]{1,0:T(8,128)(2,1)S(1)}, u32[]{:S(2)}, u32[]{:S(2)}) collective-permute-start(bf16[512,128]{1,0:T(8,128)(2,1)S(1)} %broadcast_select_fusion.3), channel_id=1, source_target_pairs={{0,64},{64,0},{1,65},{65,1},{2,66},{66,2},{3,67},{67,3},{4,68},{68... | collective-permute-start | bytes 393224 | tf_op jit(solution)/shard_map/ppermute | solution.py:172
  185.3 38.4 %collective-permute-start.7 = (bf16[512,128]{1,0:T(8,128)(2,1)S(1)}, bf16[512,128]{1,0:T(8,128)(2,1)S(1)}, u32[]{:S(2)}, u32[]{:S(2)}) collective-permute-start(bf16[512,128]{1,0:T(8,128)(2,1)S(1)} %get-tuple-element.37), channel_id=1, source_target_pairs={{8,519},{9,520},{10,521},{11,522},{12,523},{13,524},{14,525},{15,5... | collective-permute-start | bytes 393224 | tf_op jit(solution)/shard_map/ppermute | solution.py:209
  186.6 37.1 %collective-permute-start.8 = (bf16[512,128]{1,0:T(8,128)(2,1)S(1)}, bf16[512,128]{1,0:T(8,128)(2,1)S(1)}, u32[]{:S(2)}, u32[]{:S(2)}) collective-permute-start(bf16[512,128]{1,0:T(8,128)(2,1)S(1)} %get-tuple-element.37), channel_id=1, source_target_pairs={{0,513},{1,514},{2,515},{3,516},{4,517},{5,518},{6,519},{7,520},{1... | collective-permute-start | bytes 393224 | tf_op jit(solution)/shard_map/ppermute | solution.py:210
  223.7 7.1 %collective-permute-start.12 = (bf16[512,128]{1,0:T(8,128)(2,1)S(1)}, bf16[512,128]{1,0:T(8,128)(2,1)S(1)}, u32[]{:S(2)}, u32[]{:S(2)}) collective-permute-start(bf16[512,128]{1,0:T(8,128)(2,1)S(1)} %collective-permute-done.7), channel_id=1, source_target_pairs={{519,520},{520,521},{521,522},{522,523},{523,524},{524,525},{525,5... | collective-permute-start | bytes 393224 | tf_op jit(solution)/shard_map/ppermute | solution.py:227
  225.6 5.1 %collective-permute-start.13 = (bf16[512,128]{1,0:T(8,128)(2,1)S(1)}, bf16[512,128]{1,0:T(8,128)(2,1)S(1)}, u32[]{:S(2)}, u32[]{:S(2)}) collective-permute-start(bf16[512,128]{1,0:T(8,128)(2,1)S(1)} %collective-permute-done.8), channel_id=1, source_target_pairs={{513,512},{514,513},{515,514},{516,515},{517,516},{518,517},{519,5... | collective-permute-start | bytes 393224 | tf_op jit(solution)/shard_map/ppermute | solution.py:228
  230.7 3.2 %collective-permute-start.14 = (bf16[512,128]{1,0:T(8,128)(2,1)S(1)}, bf16[512,128]{1,0:T(8,128)(2,1)S(1)}, u32[]{:S(2)}, u32[]{:S(2)}) collective-permute-start(bf16[512,128]{1,0:T(8,128)(2,1)S(1)} %broadcast_select_fusion.2), channel_id=1, source_target_pairs={{0,64},{64,0},{1,65},{65,1},{2,66},{66,2},{3,67},{67,3},{4,68},{68... | collective-permute-start | bytes 393224 | tf_op jit(solution)/shard_map/ppermute | solution.py:172
  (3 other events, 2.8 us)
where the time goes:
time: 259 us; the launch traced here: 257 us
  waiting for transfers between devices  99.2 us (38%)
  blocking collectives  57.7 us (22%)
  starting transfers between devices  50.2 us (19%)
  Pallas kernels  25.7 us (10%)
  local copies, waits for them, and re-layouts  13 us (5%)
  other arithmetic  10.6 us (4%)
    all_to_all x2, blocking collectives, exchange(): return lax.all_to_all(x, axes, 0, 0, tiled=True)  57.7 us
    ppermute x2, waiting for transfers between devices, layer(): ups.append(lax.ppermute(part, RING, [(i, i + 15) for i in range(8, 16)]))  46.8 us
    all_to_all x4, starting transfers between devices, exchange(): return lax.all_to_all(x, axes, 0, 0, tiled=True)  23.1 us
    all_to_all x4, waiting for transfers between devices, exchange(): return lax.all_to_all(x, axes, 0, 0, tiled=True)  21.9 us
    ppermute x3, waiting for transfers between devices, layer(): rows.append(lax.ppermute(n, 'x', [(i, (i + s) % 4) for i in range(4)]))  20.2 us
    pallas_call x2, Pallas kernels, attend_more(): pl.pallas_call(kernel, grid=(1024 // QB,), out_shape=out if last else STA...  12.4 us
    ppermute x3, starting transfers between devices, layer(): rows.append(lax.ppermute(n, 'x', [(i, (i + s) % 4) for i in range(4)]))  9.55 us
    ppermute x2, waiting for transfers between devices, layer(): up = lax.ppermute(ups[k], RING, [(i, i + 1) for i in range(23, 31)])  8.92 us
  transfers between devices with their start and end apart: 19, of which 10 were waited for; matrix products, arithmetic and copies ran while one was open for 6% of the time, Pallas kernels for 4%

commit v1 on v0

--- a/solution.py
+++ b/solution.py
@@ -13,7 +13,7 @@
 SCALE = HEAD ** (-0.5)
 NEG = -1e30
 QB = 256
-CHUNKS = 2
+CHUNKS = 1
 STEP = 1024 // CHUNKS
 AXES = ("zh", "x", "c", "y", "zf", "zn")
 RING = ("zh", "zf", "zn")
@@ -30,24 +30,23 @@
     return lax.all_to_all(x, axes, 0, 0, tiled=True)
 
 
-def spread(x, axes, n):
-    return exchange(jnp.broadcast_to(x[None], (n,) + x.shape), axes)
-
-
-def pick(x, index):
+def pick_spread(x, index, copies, axes):
     n = index.shape[0]
 
     def kernel(i_ref, x_ref, o_ref):
         for k in range(n):
-            o_ref[k] = x_ref[i_ref[k]]
-
-    return pl.pallas_call(
-        kernel,
-        out_shape=jax.ShapeDtypeStruct((n,) + x.shape[1:], x.dtype),
+            piece = x_ref[i_ref[k]]
+            for j in range(copies):
+                o_ref[j, k] = piece
+
+    many = pl.pallas_call(
+        kernel,
+        out_shape=jax.ShapeDtypeStruct((copies, n) + x.shape[1:], x.dtype),
         in_specs=[SM, VM],
         out_specs=VM,
         name="pick",
     )(index, x)
+    return exchange(many, axes)
 
 
 def tables(zh, c):
@@ -65,20 +64,39 @@
 
 
 def project(place, mine, other, w, cos, sin):
-    def kernel(p_ref, a0, a1, a2, a3, b_ref, w_ref, cos_ref, sin_ref, o_ref):
-        for k in range(8):
-            s = k % 4
-            piece = (a0, a1, a2, a3)[s][...] if k < 4 else b_ref[s]
-            raw = jnp.dot(piece, w_ref[...], preferred_element_type=jnp.float32)
-            rows = pl.ds(pl.multiple_of(p_ref[k] * 128, 128), 128)
-            turned = raw * cos_ref[rows, :] + pltpu.roll(raw, 64, 1) * sin_ref[rows, :]
-            o_ref[rows, :] = turned.astype(jnp.bfloat16)
+    def kernel(p_ref, a0, a1, a2, a3, b_ref, w_ref, cos_ref, sin_ref, o_ref, rows, wv, cv, sv, sems):
+        pairs = [(w_ref, wv)]
+        pairs += [(a, rows.at[0, pl.ds(128 * k, 128)]) for k, a in enumerate((a0, a1, a2, a3))]
+        pairs += [(cos_ref, cv), (sin_ref, sv), (b_ref, rows.at[1])]
+        copies = [pltpu.make_async_copy(s, d, sems.at[k]) for k, (s, d) in enumerate(pairs)]
+        for copy in copies:
+            copy.start()
+        for copy in copies[:5]:
+            copy.wait()
+        for g in range(2):
+            raw = jnp.dot(rows[g], wv[...], preferred_element_type=jnp.float32)
+            for copy in copies[5:7] if g == 0 else []:
+                copy.wait()
+            for k in range(4):
+                part = raw[128 * k : 128 * (k + 1)]
+                to = pl.ds(pl.multiple_of(p_ref[4 * g + k] * 128, 128), 128)
+                turned = part * cv[to, :] + pltpu.roll(part, 64, 1) * sv[to, :]
+                o_ref[to, :] = turned.astype(jnp.bfloat16)
+            if g == 0:
+                copies[7].wait()
 
     return pl.pallas_call(
         kernel,
         out_shape=jax.ShapeDtypeStruct((1024, HEAD), jnp.bfloat16),
-        in_specs=[SM] + [VM] * 8,
+        in_specs=[SM] + [pl.BlockSpec(memory_space=pl.ANY)] * 8,
         out_specs=VM,
+        scratch_shapes=[
+            pltpu.VMEM((2, 512, 2048), jnp.bfloat16),
+            pltpu.VMEM((2048, HEAD), jnp.bfloat16),
+            pltpu.VMEM((1024, HEAD), jnp.float32),
+            pltpu.VMEM((1024, HEAD), jnp.float32),
+            pltpu.SemaphoreType.DMA((8,)),
+        ],
         name="project",
     )(place, *mine, other, w, cos, sin)
 
@@ -183,20 +201,17 @@
     w = w.reshape(2, 16, 8, 4, HEAD).transpose(3, 0, 1, 2, 4).reshape(128, 8, HEAD)
     w = exchange(w, ("x", "c", "y", "zn"))
     here = lax.dynamic_slice_in_dim(own_y * 4 + own_zn, zh * 8, 8)
-    w = pick(w, block8 * 16 + here)
-
     rows = [n]
     for s in (1, 2, 3):
         rows.append(lax.ppermute(n, "x", [(i, (i + s) % 4) for i in range(4)]))
 
-    w = spread(w, ("zh", "zf"), 8)
+    w = pick_spread(w, block8 * 16 + here, 8, ("zh", "zf"))
     block16 = jnp.arange(16, dtype=jnp.int32)
-    w = pick(w.reshape(64, 8, HEAD), ((block16 // 8) * 4 + own_zf) * 8 + block16 % 8)
-
-    other = swap_cores(jnp.stack(rows))
-
-    w = spread(w, ("y", "zn"), 16).reshape(16, 16, 8, HEAD)
+    index = ((block16 // 8) * 4 + own_zf) * 8 + block16 % 8
+    w = pick_spread(w.reshape(64, 8, HEAD), index, 16, ("y", "zn"))
     w = w.transpose(1, 0, 2, 3).reshape(2048, HEAD)
+
+    other = swap_cores(jnp.concatenate(rows))
 
     chip = (x - jnp.arange(4, dtype=jnp.int32)) % 4
     place = jnp.concatenate([chip * 2 + c, chip * 2 + 1 - c])

time: 259 us -> 237 us (0.915)
  waiting for transfers between devices: 99.2 us -> 90.3 us
  starting transfers between devices: 50.2 us -> 43.6 us
  local copies, waits for them, and re-layouts: 13 us -> 9.36 us
  Pallas kernels: 25.7 us -> 23.1 us
    ppermute x2 -> x1, waiting for transfers between devices: 46.8 us -> 41.9 us  [layer(): ups.append(lax.ppermute(part, RING, [(i, i + 15) for i in range(8, 16)]))]
    pallas_call x2 -> x1, Pallas kernels: 12.4 us -> 8.2 us  [attend_more(): pl.pallas_call(kernel, grid=(1024 // QB,), out_shape=out if last else STA...]
    ppermute x4 -> x3, starting transfers between devices: 8.28 us -> 6.23 us  [swap_cores(): return lax.ppermute(x, 'c', [(0, 1), (1, 0)])]
    ppermute x2 -> x1, waiting for transfers between devices: 8.92 us -> 7.21 us  [layer(): up = lax.ppermute(ups[k], RING, [(i, i + 1) for i in range(23, 31)])]
  transfers between devices with their start and end apart: 19 -> 14, of which waited for: 10 -> 8; matrix products, arithmetic and copies ran while one was open for 6% -> 5% of each run, Pallas kernels for 4% -> 2%
where the time goes in v1:
time: 237 us; the launch traced here: 236 us
  waiting for transfers between devices  90.3 us (38%)
  blocking collectives  58.3 us (25%)
  starting transfers between devices  43.6 us (18%)
  Pallas kernels  23.1 us (10%)
  other arithmetic  9.96 us (4%)
  local copies, waits for them, and re-layouts  9.36 us (4%)
    all_to_all x2, blocking collectives, exchange(): return lax.all_to_all(x, axes, 0, 0, tiled=True)  58.3 us
    ppermute x1, waiting for transfers between devices, layer(): ups.append(lax.ppermute(part, RING, [(i, i + 15) for i in range(8, 16)]))  41.9 us
    all_to_all x4, starting transfers between devices, exchange(): return lax.all_to_all(x, axes, 0, 0, tiled=True)  23.3 us
    ppermute x3, waiting for transfers between devices, layer(): rows.append(lax.ppermute(n, 'x', [(i, (i + s) % 4) for i in range(4)]))  20.2 us
    all_to_all x4, waiting for transfers between devices, exchange(): return lax.all_to_all(x, axes, 0, 0, tiled=True)  19.4 us
    ppermute x3, starting transfers between devices, layer(): rows.append(lax.ppermute(n, 'x', [(i, (i + s) % 4) for i in range(4)]))  9.55 us
    pallas_call x1, Pallas kernels, attend_more(): pl.pallas_call(kernel, grid=(1024 // QB,), out_shape=out if last else STA...  8.2 us
    ppermute x1, waiting for transfers between devices, layer(): up = lax.ppermute(ups[k], RING, [(i, i + 1) for i in range(23, 31)])  7.21 us
  transfers between devices with their start and end apart: 14, of which 8 were waited for; matrix products, arithmetic and copies ran while one was open for 5% of the time, Pallas kernels for 2%

profile of v1, /device:TPU:960, one launch (start us, length us, event | category | flops | bytes accessed | tf_op | source)
XLA Modules:
  0.0 235.5 jit_solution(14886097596094183890)
XLA Ops:
  2.4 11.1 %all-to-all-start = ((bf16[128,8,128]{2,1,0:T(8,128)(2,1)}), bf16[128,8,128]{2,1,0:T(8,128)(2,1)S(1)}, u32[]{:S(2)}, u32[]{:S(2)}) async-start(bf16[128,8,128]{2,1,0:T(8,128)(2,1)} %bitcast.3), calls=%async_computation | async-start | bytes 524288 | tf_op jit(solution)/shard_map/all_to_all | solution.py:30
  15.3 9.6 %all-to-all-done.x_ref = bf16[128,8,128]{2,1,0:T(8,128)(2,1)S(1)} async-done(((bf16[128,8,128]{2,1,0:T(8,128)(2,1)}), bf16[128,8,128]{2,1,0:T(8,128)(2,1)S(1)}, u32[]{:S(2)}, u32[]{:S(2)}) %all-to-all-start) | async-done | bytes 262176 | tf_op jit(solution)/shard_map/all_to_all | solution.py:30
  27.3 43.1 %all_to_all.30 = bf16[8,8,8,128]{3,2,1,0:T(8,128)(2,1)} all-to-all(bf16[8,8,8,128]{3,2,1,0:T(8,128)(2,1)} %pick.2), channel_id=1, replica_groups=mesh['zh'=2,'x'=4,'c'=2,'y'=4,'zf'=4,'zn'=4] {'zh','zf'}, dimensions={0} | all-to-all | bytes 262144 | tf_op jit(solution)/shard_map/all_to_all | solution.py:30
  72.2 4.6 %all-to-all-start.2 = ((bf16[16,16,8,128]{3,2,1,0:T(8,128)(2,1)}), bf16[16,16,8,128]{3,2,1,0:T(8,128)(2,1)S(1)}, u32[]{:S(2)}, u32[]{:S(2)}) async-start(bf16[16,16,8,128]{3,2,1,0:T(8,128)(2,1)} %pick.3), calls=%async_computation.2 | async-start | bytes 1048576 | tf_op jit(solution)/shard_map/all_to_all | solution.py:30
  76.8 2.5 %collective-permute-start = (bf16[128,2048]{1,0:T(8,128)(2,1)S(1)}, bf16[128,2048]{1,0:T(8,128)(2,1)S(1)}, u32[]{:S(2)}, u32[]{:S(2)}) collective-permute-start(bf16[128,2048]{1,0:T(8,128)(2,1)S(1)} %bitcast.40), channel_id=1, source_target_pairs={{0,128},{128,256},{256,384},{384,0},{1,129},{129,257},{257,385},{3... | collective-permute-start | bytes 1572872 | tf_op jit(solution)/shard_map/ppermute | solution.py:206
  79.3 3.5 %collective-permute-start.1 = (bf16[128,2048]{1,0:T(8,128)(2,1)S(1)}, bf16[128,2048]{1,0:T(8,128)(2,1)S(1)}, u32[]{:S(2)}, u32[]{:S(2)}) collective-permute-start(bf16[128,2048]{1,0:T(8,128)(2,1)S(1)} %bitcast.41), channel_id=1, source_target_pairs={{0,256},{128,384},{256,0},{384,128},{1,257},{129,385},{257,1},{385... | collective-permute-start | bytes 1572872 | tf_op jit(solution)/shard_map/ppermute | solution.py:206
  82.9 3.5 %collective-permute-start.2 = (bf16[128,2048]{1,0:T(8,128)(2,1)S(1)}, bf16[128,2048]{1,0:T(8,128)(2,1)S(1)}, u32[]{:S(2)}, u32[]{:S(2)}) collective-permute-start(bf16[128,2048]{1,0:T(8,128)(2,1)S(1)} %bitcast.42), channel_id=1, source_target_pairs={{0,384},{128,0},{256,128},{384,256},{1,385},{129,1},{257,129},{385... | collective-permute-start | bytes 1572872 | tf_op jit(solution)/shard_map/ppermute | solution.py:206
  86.4 17.7 %collective-permute-done.a1 = bf16[128,2048]{1,0:T(8,128)(2,1)S(1)} collective-permute-done((bf16[128,2048]{1,0:T(8,128)(2,1)S(1)}, bf16[128,2048]{1,0:T(8,128)(2,1)S(1)}, u32[]{:S(2)}, u32[]{:S(2)}) %collective-permute-start) | collective-permute-done | bytes 524320 | tf_op jit(solution)/shard_map/ppermute | solution.py:206
  104.1 2.5 %collective-permute-done.2.a3 = bf16[128,2048]{1,0:T(8,128)(2,1)S(1)} collective-permute-done((bf16[128,2048]{1,0:T(8,128)(2,1)S(1)}, bf16[128,2048]{1,0:T(8,128)(2,1)S(1)}, u32[]{:S(2)}, u32[]{:S(2)}) %collective-permute-start.2) | collective-permute-done | bytes 524320 | tf_op jit(solution)/shard_map/ppermute | solution.py:206
  109.0 1.9 collective-permute-start.3
  111.6 1.9 fusion
  117.1 5.9 %project.1 = bf16[1024,128]{1,0:T(8,128)(2,1)} custom-call(s32[8]{0:T(128)} %pad_add_fusion.p_ref, bf16[128,2048]{1,0:T(8,128)(2,1)} %bitcast.39, bf16[128,2048]{1,0:T(8,128)(2,1)} %copy-done.4, bf16[128,2048]{1,0:T(8,128)(2,1)} %copy-done.5, bf16[128,2048]{1,0:T(8,128)(2,1)} %copy-done.6, bf16[512,2048]{1,0:T(8,128)(2,1)} %copy-done.2, ...), custom_call_target="tpu_custom_call" | custom-call | tf_op jit(solution)/shard_map/project/pallas_call | solution.py:88
  123.0 4.2 %all-to-all-start.4 = ((bf16[8,128,128]{2,1,0:T(8,128)(2,1)}), bf16[8,128,128]{2,1,0:T(8,128)(2,1)S(1)}, u32[]{:S(2)}, u32[]{:S(2)}) async-start(bf16[8,128,128]{2,1,0:T(8,128)(2,1)} %bitcast.33), calls=%async_computation.4 | async-start | bytes 524288 | tf_op jit(solution)/shard_map/all_to_all | solution.py:30
  127.2 2.4 %collective-permute-start.6 = (bf16[1024,128]{1,0:T(8,128)(2,1)}, bf16[1024,128]{1,0:T(8,128)(2,1)S(1)}, u32[]{:S(2)}, u32[]{:S(2)}) collective-permute-start(bf16[1024,128]{1,0:T(8,128)(2,1)} %project.1), channel_id=1, source_target_pairs={{0,64},{64,0},{1,65},{65,1},{2,66},{66,2},{3,67},{67,3},{4,68},{68... | collective-permute-start | bytes 786440 | tf_op jit(solution)/shard_map/ppermute | solution.py:190
  132.6 2.1 all-to-all-done.4
  134.7 3.5 %all-to-all-start.3 = ((bf16[8,128,256]{2,1,0:T(8,128)(2,1)}), bf16[8,128,256]{2,1,0:T(8,128)(2,1)S(1)}, u32[]{:S(2)}, u32[]{:S(2)}) async-start(bf16[8,128,256]{2,1,0:T(8,128)(2,1)} %bitcast.28), calls=%async_computation.3 | async-start | bytes 1048576 | tf_op jit(solution)/shard_map/all_to_all | solution.py:30
  140.7 7.7 %all-to-all-done.3 = bf16[8,128,256]{2,1,0:T(8,128)(2,1)S(1)} async-done(((bf16[8,128,256]{2,1,0:T(8,128)(2,1)}), bf16[8,128,256]{2,1,0:T(8,128)(2,1)S(1)}, u32[]{:S(2)}, u32[]{:S(2)}) %all-to-all-start.3) | async-done | bytes 524320 | tf_op jit(solution)/shard_map/all_to_all | solution.py:30
  149.2 5.6 %attend_own.1 = (f32[1024,256]{1,0:T(8,128)}, f32[1024,4]{1,0:T(8,128)}) custom-call(bf16[1024,256]{1,0:T(8,128)(2,1)} %bitcast.31, bf16[1024,128]{1,0:T(8,128)(2,1)} %get-tuple-element.22.k_ref, bf16[1024,128]{1,0:T(8,128)(2,1)} %get-tuple-element.21.v_ref), custom_call_target="tpu_custom_call" | custom-call | tf_op jit(solution)/shard_map/attend_own/pallas_call | solution.py:127
  154.8 41.9 %collective-permute-done.4 = bf16[1024,128]{1,0:T(8,128)(2,1)S(1)} collective-permute-done((bf16[1024,128]{1,0:T(8,128)(2,1)S(1)}, bf16[1024,128]{1,0:T(8,128)(2,1)S(1)}, u32[]{:S(2)}, u32[]{:S(2)}) %collective-permute-start.4) | collective-permute-done | bytes 262176 | tf_op jit(solution)/shard_map/ppermute | solution.py:224
  196.7 1.9 collective-permute-start.7
  199.3 7.2 %collective-permute-done.7 = bf16[1024,128]{1,0:T(8,128)(2,1)S(1)} collective-permute-done((bf16[1024,128]{1,0:T(8,128)(2,1)S(1)}, bf16[1024,128]{1,0:T(8,128)(2,1)S(1)}, u32[]{:S(2)}, u32[]{:S(2)}) %collective-permute-start.7) | collective-permute-done | bytes 262176 | tf_op jit(solution)/shard_map/ppermute | solution.py:242
  206.5 1.9 collective-permute-start.9
  210.8 8.2 %attend_more.1 = bf16[1024,256]{1,0:T(8,128)(2,1)} custom-call(s32[1]{0:T(128)} %bitcast.15.z_ref, bf16[1024,256]{1,0:T(8,128)(2,1)} %bitcast.32, bf16[1024,128]{1,0:T(8,128)(2,1)} %get-tuple-element.20.k_ref, bf16[1024,128]{1,0:T(8,128)(2,1)} %get-tuple-element.19.v_ref, f32[1024,256]{1,0:T(8,128)} %get-tuple-element.17.acc_ref, ...), custom_call_target="tpu_custom_call" | custom-call | tf_op jit(solution)/shard_map/attend_more/pallas_call | solution.py:179
  219.0 15.2 %all_to_all.31 = bf16[8,128,256]{2,1,0:T(8,128)(2,1)S(1)} all-to-all(bf16[8,128,256]{2,1,0:T(8,128)(2,1)} %bitcast.38), channel_id=1, replica_groups=mesh['zh'=2,'x'=4,'c'=2,'y'=4,'zf'=4,'zn'=4] {'x','c'}, dimensions={0} | all-to-all | bytes 1048576 | tf_op jit(solution)/shard_map/all_to_all | solution.py:30
  (53 shorter events, 25.0 us)
Async XLA Ops:
  0.6 76.2 %copy-start.3 = (bf16[1,128,2048]{2,1,0:T(8,128)(2,1)S(1)}, bf16[1,128,2048]{2,1,0:T(8,128)(2,1)}, u32[]{:S(2)}) copy-start(bf16[1,128,2048]{2,1,0:T(8,128)(2,1)} %param.6) | copy-start | bytes 1572868
  2.4 22.5 %all-to-all-start = ((bf16[128,8,128]{2,1,0:T(8,128)(2,1)}), bf16[128,8,128]{2,1,0:T(8,128)(2,1)S(1)}, u32[]{:S(2)}, u32[]{:S(2)}) async-start(bf16[128,8,128]{2,1,0:T(8,128)(2,1)} %bitcast.3), calls=%async_computation | async-start | bytes 524288 | tf_op jit(solution)/shard_map/all_to_all | solution.py:30
  24.9 0.7 copy-start.7
  72.2 42.6 %all-to-all-start.2 = ((bf16[16,16,8,128]{3,2,1,0:T(8,128)(2,1)}), bf16[16,16,8,128]{3,2,1,0:T(8,128)(2,1)S(1)}, u32[]{:S(2)}, u32[]{:S(2)}) async-start(bf16[16,16,8,128]{3,2,1,0:T(8,128)(2,1)} %pick.3), calls=%async_computation.2 | async-start | bytes 1048576 | tf_op jit(solution)/shard_map/all_to_all | solution.py:30
  76.8 27.3 %collective-permute-start = (bf16[128,2048]{1,0:T(8,128)(2,1)S(1)}, bf16[128,2048]{1,0:T(8,128)(2,1)S(1)}, u32[]{:S(2)}, u32[]{:S(2)}) collective-permute-start(bf16[128,2048]{1,0:T(8,128)(2,1)S(1)} %bitcast.40), channel_id=1, source_target_pairs={{0,128},{128,256},{256,384},{384,0},{1,129},{129,257},{257,385},{3... | collective-permute-start | bytes 1572872 | tf_op jit(solution)/shard_map/ppermute | solution.py:206
  79.3 24.8 %collective-permute-start.1 = (bf16[128,2048]{1,0:T(8,128)(2,1)S(1)}, bf16[128,2048]{1,0:T(8,128)(2,1)S(1)}, u32[]{:S(2)}, u32[]{:S(2)}) collective-permute-start(bf16[128,2048]{1,0:T(8,128)(2,1)S(1)} %bitcast.41), channel_id=1, source_target_pairs={{0,256},{128,384},{256,0},{384,128},{1,257},{129,385},{257,1},{385... | collective-permute-start | bytes 1572872 | tf_op jit(solution)/shard_map/ppermute | solution.py:206
  82.9 23.7 %collective-permute-start.2 = (bf16[128,2048]{1,0:T(8,128)(2,1)S(1)}, bf16[128,2048]{1,0:T(8,128)(2,1)S(1)}, u32[]{:S(2)}, u32[]{:S(2)}) collective-permute-start(bf16[128,2048]{1,0:T(8,128)(2,1)S(1)} %bitcast.42), channel_id=1, source_target_pairs={{0,384},{128,0},{256,128},{384,256},{1,385},{129,1},{257,129},{385... | collective-permute-start | bytes 1572872 | tf_op jit(solution)/shard_map/ppermute | solution.py:206
  104.1 2.5 %copy-start.4 = (bf16[128,2048]{1,0:T(8,128)(2,1)}, bf16[128,2048]{1,0:T(8,128)(2,1)S(1)}, u32[]{:S(2)}) copy-start(bf16[128,2048]{1,0:T(8,128)(2,1)S(1)} %collective-permute-done.a1) | copy-start | bytes 1572868
  104.1 2.5 %copy-start.5 = (bf16[128,2048]{1,0:T(8,128)(2,1)}, bf16[128,2048]{1,0:T(8,128)(2,1)S(1)}, u32[]{:S(2)}) copy-start(bf16[128,2048]{1,0:T(8,128)(2,1)S(1)} %collective-permute-done.1.a2) | copy-start | bytes 1572868
  106.6 0.8 copy-start.6
  109.0 6.7 %collective-permute-start.3 = (bf16[512,2048]{1,0:T(8,128)(2,1)}, bf16[512,2048]{1,0:T(8,128)(2,1)S(1)}, u32[]{:S(2)}, u32[]{:S(2)}) collective-permute-start(bf16[512,2048]{1,0:T(8,128)(2,1)} %pad_maximum_fusion), channel_id=1, source_target_pairs={{0,64},{64,0},{1,65},{65,1},{2,66},{66,2},{3,67},{67,3},{4,68},{68... | collective-permute-start | bytes 6291464 | tf_op jit(solution)/shard_map/ppermute | solution.py:190
  115.8 1.4 copy-start.2
  117.1 12.5 %copy-start.8 = (bf16[1,128,2048]{2,1,0:T(8,128)(2,1)S(1)}, bf16[1,128,2048]{2,1,0:T(8,128)(2,1)}, u32[]{:S(2)}) copy-start(bf16[1,128,2048]{2,1,0:T(8,128)(2,1)} %param.5) | copy-start | bytes 1572868
  123.0 7.6 %copy-start.1 = (bf16[1024,128]{1,0:T(8,128)(2,1)S(1)}, bf16[1024,128]{1,0:T(8,128)(2,1)}, u32[]{:S(2)}) copy-start(bf16[1024,128]{1,0:T(8,128)(2,1)} %project.1) | copy-start | bytes 786436
  123.0 11.7 %all-to-all-start.4 = ((bf16[8,128,128]{2,1,0:T(8,128)(2,1)}), bf16[8,128,128]{2,1,0:T(8,128)(2,1)S(1)}, u32[]{:S(2)}, u32[]{:S(2)}) async-start(bf16[8,128,128]{2,1,0:T(8,128)(2,1)} %bitcast.33), calls=%async_computation.4 | async-start | bytes 524288 | tf_op jit(solution)/shard_map/all_to_all | solution.py:30
  127.2 12.7 %collective-permute-start.6 = (bf16[1024,128]{1,0:T(8,128)(2,1)}, bf16[1024,128]{1,0:T(8,128)(2,1)S(1)}, u32[]{:S(2)}, u32[]{:S(2)}) collective-permute-start(bf16[1024,128]{1,0:T(8,128)(2,1)} %project.1), channel_id=1, source_target_pairs={{0,64},{64,0},{1,65},{65,1},{2,66},{66,2},{3,67},{67,3},{4,68},{68... | collective-permute-start | bytes 786440 | tf_op jit(solution)/shard_map/ppermute | solution.py:190
  130.6 66.1 %collective-permute-start.4 = (bf16[1024,128]{1,0:T(8,128)(2,1)S(1)}, bf16[1024,128]{1,0:T(8,128)(2,1)S(1)}, u32[]{:S(2)}, u32[]{:S(2)}) collective-permute-start(bf16[1024,128]{1,0:T(8,128)(2,1)S(1)} %copy-done.1), channel_id=1, source_target_pairs={{8,519},{9,520},{10,521},{11,522},{12,523},{13,524},{14,525},{15,5... | collective-permute-start | bytes 786440 | tf_op jit(solution)/shard_map/ppermute | solution.py:224
  131.9 64.8 %collective-permute-start.5 = (bf16[1024,128]{1,0:T(8,128)(2,1)S(1)}, bf16[1024,128]{1,0:T(8,128)(2,1)S(1)}, u32[]{:S(2)}, u32[]{:S(2)}) collective-permute-start(bf16[1024,128]{1,0:T(8,128)(2,1)S(1)} %copy-done.1), channel_id=1, source_target_pairs={{0,513},{1,514},{2,515},{3,516},{4,517},{5,518},{6,519},{7,520},{1... | collective-permute-start | bytes 786440 | tf_op jit(solution)/shard_map/ppermute | solution.py:225
  134.7 13.7 %all-to-all-start.3 = ((bf16[8,128,256]{2,1,0:T(8,128)(2,1)}), bf16[8,128,256]{2,1,0:T(8,128)(2,1)S(1)}, u32[]{:S(2)}, u32[]{:S(2)}) async-start(bf16[8,128,256]{2,1,0:T(8,128)(2,1)} %bitcast.28), calls=%async_computation.3 | async-start | bytes 1048576 | tf_op jit(solution)/shard_map/all_to_all | solution.py:30
  148.4 0.8 copy-start
  196.7 9.8 %collective-permute-start.7 = (bf16[1024,128]{1,0:T(8,128)(2,1)S(1)}, bf16[1024,128]{1,0:T(8,128)(2,1)S(1)}, u32[]{:S(2)}, u32[]{:S(2)}) collective-permute-start(bf16[1024,128]{1,0:T(8,128)(2,1)S(1)} %collective-permute-done.4), channel_id=1, source_target_pairs={{519,520},{520,521},{521,522},{522,523},{523,524},{524,525},{525,5... | collective-permute-start | bytes 786440 | tf_op jit(solution)/shard_map/ppermute | solution.py:242
  198.6 7.9 %collective-permute-start.8 = (bf16[1024,128]{1,0:T(8,128)(2,1)S(1)}, bf16[1024,128]{1,0:T(8,128)(2,1)S(1)}, u32[]{:S(2)}, u32[]{:S(2)}) collective-permute-start(bf16[1024,128]{1,0:T(8,128)(2,1)S(1)} %collective-permute-done.5), channel_id=1, source_target_pairs={{513,512},{514,513},{515,514},{516,515},{517,516},{518,517},{519,5... | collective-permute-start | bytes 786440 | tf_op jit(solution)/shard_map/ppermute | solution.py:243
  206.5 3.4 %collective-permute-start.9 = (bf16[1024,128]{1,0:T(8,128)(2,1)S(1)}, bf16[1024,128]{1,0:T(8,128)(2,1)S(1)}, u32[]{:S(2)}, u32[]{:S(2)}) collective-permute-start(bf16[1024,128]{1,0:T(8,128)(2,1)S(1)} %broadcast_select_fusion), channel_id=1, source_target_pairs={{0,64},{64,0},{1,65},{65,1},{2,66},{66,2},{3,67},{67,3},{4,68},{68... | collective-permute-start | bytes 786440 | tf_op jit(solution)/shard_map/ppermute | solution.py:190

commit v2 on v1

v2 whole, which is shorter than its diff:
```python
import math

import jax
import jax.numpy as jnp
from jax import lax
from jax.experimental import pallas as pl
from jax.experimental.pallas import tpu as pltpu
from jax.sharding import Mesh
from jax.sharding import PartitionSpec as P


HEAD = 128
SCALE = HEAD ** (-0.5)
SCALE2 = SCALE * math.log2(math.e)
NEG = -1e30
QB = 256
AXES = ("zh", "x", "c", "y", "zf", "zn")
RING = ("zh", "zf", "zn")
VM = pl.BlockSpec(memory_space=pltpu.VMEM)
SM = pl.BlockSpec(memory_space=pltpu.SMEM)
NT = (((1,), (1,)), ((), ()))
STATE = (
    jax.ShapeDtypeStruct((1024, 256), jnp.float32),
    jax.ShapeDtypeStruct((1024, 4), jnp.float32),
)


def exchange(x, axes):
    return lax.all_to_all(x, axes, 0, 0, tiled=True)


def pick_spread(x, index, copies, axes):
    n = index.shape[0]

    def kernel(i_ref, x_ref, o_ref):
        for k in range(n):
            piece = x_ref[i_ref[k]]
            for j in range(copies):
                o_ref[j, k] = piece

    many = pl.pallas_call(
        kernel,
        out_shape=jax.ShapeDtypeStruct((copies, n) + x.shape[1:], x.dtype),
        in_specs=[SM, VM],
        out_specs=VM,
        name="pick",
    )(index, x)
    return exchange(many, axes)


def tables(zh, c):
    half = HEAD // 2
    freq = jnp.exp(
        jnp.arange(half).astype(jnp.float32) * (-2.0 * math.log(500000.0) / HEAD)
    )
    t = zh * 1024 + jnp.arange(1024, dtype=jnp.int32)
    angles = t.astype(jnp.float32)[:, None] * freq[None, :]
    cos, sin = jnp.cos(angles), jnp.sin(angles)
    cos = jnp.concatenate([cos, cos], axis=1)
    sin = jnp.concatenate([-sin, sin], axis=1)
    is_key = c == 0
    return jnp.where(is_key, cos, 1.0), jnp.where(is_key, sin, 0.0)


def turn(place, mine, other, cos, sin):
    def kernel(p_ref, a_ref, b_ref, cos_ref, sin_ref, o_ref):
        for k in range(8):
            part = (a_ref if k < 4 else b_ref)[pl.ds(128 * (k % 4), 128), :]
            to = pl.ds(pl.multiple_of(p_ref[k] * 128, 128), 128)
            turned = part * cos_ref[to, :] + pltpu.roll(part, 64, 1) * sin_ref[to, :]
            o_ref[to, :] = turned.astype(jnp.bfloat16)

    return pl.pallas_call(
        kernel,
        out_shape=jax.ShapeDtypeStruct((1024, HEAD), jnp.bfloat16),
        in_specs=[SM] + [VM] * 4,
        out_specs=VM,
        name="turn",
    )(place, mine, other, cos, sin)


def attend_own(q, k, v):
    def kernel(q_ref, k_ref, v_ref, acc_ref, st_ref):
        for i in range(1024 // QB):
            rows = pl.ds(i * QB, QB)
            n = (i + 1) * QB
            r = lax.broadcasted_iota(jnp.int32, (QB, n), 0) + i * QB
            t = lax.broadcasted_iota(jnp.int32, (QB, n), 1)
            tops, totals = [], []
            for h in range(2):
                col = pl.ds(h * HEAD, HEAD)
                s = lax.dot_general(
                    q_ref[rows, col], k_ref[:n, :], NT, preferred_element_type=jnp.float32
                )
                s = jnp.where(t <= r, s, NEG)
                m = jnp.max(s, axis=1, keepdims=True)
                p = jnp.exp((s - m) * SCALE)
                tops.append(m)
                totals.append(jnp.sum(p, axis=1, keepdims=True))
                acc_ref[rows, col] = jnp.dot(
                    p.astype(jnp.bfloat16), v_ref[:n, :], preferred_element_type=jnp.float32
                )
            st_ref[rows, :] = jnp.concatenate(tops + totals, axis=1)

    return pl.pallas_call(
        kernel,
        out_shape=STATE,
        in_specs=[VM] * 3,
        out_specs=(VM,) * 2,
        name="attend_own",
    )(q, k, v)


def attend_more(who, q, first, partner, acc, st):
    part = 512

    def kernel(w_ref, q_ref, a_ref, b_ref, acc_ref, st_ref, o_ref, kv):
        @pl.when(pl.program_id(0) == 0)
        def _():
            kv[w_ref[1]] = a_ref[...]
            kv[1 - w_ref[1]] = b_ref[...]

        @pl.when(w_ref[0] == 0)
        def _():
            for h in range(2):
                col = pl.ds(h * HEAD, HEAD)
                o_ref[:, col] = (acc_ref[:, col] / st_ref[:, 2 + h : 3 + h]).astype(jnp.bfloat16)

        @pl.when(w_ref[0] != 0)
        def _():
            for h in range(2):
                col = pl.ds(h * HEAD, HEAD)
                tiles = [
                    lax.dot_general(
                        q_ref[:, col],
                        kv[0, t : t + part],
                        NT,
                        preferred_element_type=jnp.float32,
                    )
                    for t in range(0, 1024, part)
                ]
                m0 = st_ref[:, h : h + 1]
                m1 = m0
                for s in tiles:
                    m1 = jnp.maximum(m1, jnp.max(s, axis=1, keepdims=True))
                fade = jnp.exp2((m0 - m1) * SCALE2)
                total = st_ref[:, 2 + h : 3 + h] * fade
                out = acc_ref[:, col] * fade
                for t, s in enumerate(tiles):
                    p = jnp.exp2((s - m1) * SCALE2)
                    total = total + jnp.sum(p, axis=1, keepdims=True)
                    out = out + jnp.dot(
                        p.astype(jnp.bfloat16),
                        kv[1, t * part : (t + 1) * part],
                        preferred_element_type=jnp.float32,
                    )
                o_ref[:, col] = (out / total).astype(jnp.bfloat16)

    row = lambda width: pl.BlockSpec((QB, width), lambda i: (i, 0))
    whole = pl.BlockSpec((1024, HEAD), lambda i: (0, 0))
    return pl.pallas_call(
        kernel,
        grid=(1024 // QB,),
        out_shape=jax.ShapeDtypeStruct((1024, 256), jnp.bfloat16),
        in_specs=[SM, row(256), whole, whole, row(256), row(4)],
        out_specs=row(256),
        scratch_shapes=[pltpu.VMEM((2, 1024, HEAD), jnp.bfloat16)],
        name="attend_more",
    )(who, q, first, partner, acc, st)


def swap_cores(x):
    return lax.ppermute(x, "c", [(0, 1), (1, 0)])


def layer(queries, normed, key_weight_copies, value_weight_copies, owner):
    zh, x, c = lax.axis_index("zh"), lax.axis_index("x"), lax.axis_index("c")
    z_lo = lax.axis_index(("zf", "zn"))
    own_y, own_zf, own_zn = owner // 16, (owner // 4) % 4, owner % 4
    block8 = jnp.arange(8, dtype=jnp.int32)
    n = normed[0]

    w = jnp.stack([key_weight_copies[0], value_weight_copies[0]])
    w = w.reshape(2, 16, 8, 4, HEAD).transpose(3, 0, 1, 2, 4).reshape(128, 8, HEAD)
    w = exchange(w, ("x", "c", "y", "zn"))
    here = lax.dynamic_slice_in_dim(own_y * 4 + own_zn, zh * 8, 8)
    rows = [n]
    for s in (1, 2, 3):
        rows.append(lax.ppermute(n, "x", [(i, (i + s) % 4) for i in range(4)]))

    w = pick_spread(w, block8 * 16 + here, 8, ("zh", "zf"))
    block16 = jnp.arange(16, dtype=jnp.int32)
    index = ((block16 // 8) * 4 + own_zf) * 8 + block16 % 8
    w = pick_spread(w.reshape(64, 8, HEAD), index, 16, ("y", "zn"))
    w = w.transpose(1, 0, 2, 3).reshape(2048, HEAD)

    mine = jnp.concatenate(rows)
    other = swap_cores(mine)

    chip = (x - jnp.arange(4, dtype=jnp.int32)) % 4
    place = jnp.concatenate([chip * 2 + c, chip * 2 + 1 - c])
    cos, sin = tables(zh, c)
    raw = [jnp.dot(r, w, preferred_element_type=jnp.float32) for r in (mine, other)]
    kv = turn(place, *raw, cos, sin)

    up = lax.ppermute(kv, RING, [(i, i + 15) for i in range(8, 16)])
    down = lax.ppermute(kv, RING, [(i, i + 17) for i in range(8)])

    partner = swap_cores(kv)
    keys, values = jnp.where(c == 0, kv, partner), jnp.where(c == 0, partner, kv)
    q = queries[0].reshape(128, 8, 256).transpose(1, 0, 2)
    q = exchange(q, ("x", "c")).reshape(1024, 256)
    state = attend_own(q, keys, values)
    cache = exchange(kv.reshape(8, 128, HEAD), ("x", "c")).reshape(4, 2, 128, HEAD)
    cache_keys = cache[:, 0].transpose(1, 0, 2).reshape(1, 128, 512)
    cache_values = cache[:, 1].transpose(1, 0, 2).reshape(1, 128, 512)

    up, down, state, cache_keys, cache_values = lax.optimization_barrier(
        (up, down, state, cache_keys, cache_values)
    )
    up = lax.ppermute(up, RING, [(i, i + 1) for i in range(23, 31)])
    down = lax.ppermute(down, RING, [(i, i - 1) for i in range(17, 25)])
    first = jnp.where(z_lo >= 8, up, down)
    partner = swap_cores(first)
    state = attend_more(jnp.stack([zh, c]), q, first, partner, *state)
    out = exchange(state.reshape(8, 128, 256), ("x", "c"))
    attended = out.transpose(1, 0, 2).reshape(1, 128, 2048)
    return cache_keys, cache_values, attended


def solution(mesh):
    torus = Mesh(mesh.devices.reshape(2, 4, 2, 4, 4, 4), AXES)
    spec = P(("y", "zf", "zn"), ("zh", "x", "c"), None)
    return jax.shard_map(
        layer,
        mesh=torus,
        in_specs=(spec, spec, spec, spec, P()),
        out_specs=(spec, spec, spec),
        check_vma=False,
    )
```

time: 237 us -> 232 us (0.979)
  matrix products: 0 us -> 4.47 us
  Pallas kernels: 23.1 us -> 19.1 us
    dot_general x0 -> x2, matrix products: none -> 4.47 us  [layer(): jnp.dot(r, w, preferred_element_type=jnp.float32)]
    pallas_call x2, Pallas kernels: 14.1 us -> 10.1 us  [the longest x1 7.8 us: attend_more(): pl.pallas_call(kernel, grid=(1024 // QB,), out_shape=jax.ShapeDtypeStruct...]
where the time goes in v2:
time: 232 us; the launch traced here: 231 us
  waiting for transfers between devices  89.6 us (39%)
  blocking collectives  58.3 us (25%)
  starting transfers between devices  43.6 us (19%)
  Pallas kernels  19.1 us (8%)
  other arithmetic  8.32 us (4%)
  local copies, waits for them, and re-layouts  7.09 us (3%)
  matrix products  4.47 us (2%)
    all_to_all x2, blocking collectives, exchange(): return lax.all_to_all(x, axes, 0, 0, tiled=True)  58.3 us
    ppermute x1, waiting for transfers between devices, layer(): up = lax.ppermute(kv, RING, [(i, i + 15) for i in range(8, 16)])  41.9 us
    all_to_all x4, starting transfers between devices, exchange(): return lax.all_to_all(x, axes, 0, 0, tiled=True)  23.3 us
    ppermute x3, waiting for transfers between devices, layer(): rows.append(lax.ppermute(n, 'x', [(i, (i + s) % 4) for i in range(4)]))  20.2 us
    all_to_all x4, waiting for transfers between devices, exchange(): return lax.all_to_all(x, axes, 0, 0, tiled=True)  19.4 us
    ppermute x3, starting transfers between devices, layer(): rows.append(lax.ppermute(n, 'x', [(i, (i + s) % 4) for i in range(4)]))  9.55 us
    pallas_call x1, Pallas kernels, attend_more(): pl.pallas_call(kernel, grid=(1024 // QB,), out_shape=jax.ShapeDtypeStruct...  7.8 us
    ppermute x1, waiting for transfers between devices, layer(): up = lax.ppermute(up, RING, [(i, i + 1) for i in range(23, 31)])  7.21 us
  transfers between devices with their start and end apart: 14, of which 8 were waited for; matrix products, arithmetic and copies ran while one was open for 5% of the time, Pallas kernels for 2%

profile of v2, /device:TPU:960, one launch (start us, length us, event | category | flops | bytes accessed | tf_op | source)
XLA Modules:
  0.0 231.4 jit_solution(13297814222115462977)
XLA Ops:
  2.4 11.1 %all-to-all-start = ((bf16[128,8,128]{2,1,0:T(8,128)(2,1)}), bf16[128,8,128]{2,1,0:T(8,128)(2,1)S(1)}, u32[]{:S(2)}, u32[]{:S(2)}) async-start(bf16[128,8,128]{2,1,0:T(8,128)(2,1)} %bitcast.3), calls=%async_computation | async-start | bytes 524288 | tf_op jit(solution)/shard_map/all_to_all | solution.py:29
  15.4 9.5 %all-to-all-done.x_ref = bf16[128,8,128]{2,1,0:T(8,128)(2,1)S(1)} async-done(((bf16[128,8,128]{2,1,0:T(8,128)(2,1)}), bf16[128,8,128]{2,1,0:T(8,128)(2,1)S(1)}, u32[]{:S(2)}, u32[]{:S(2)}) %all-to-all-start) | async-done | bytes 262176 | tf_op jit(solution)/shard_map/all_to_all | solution.py:29
  27.3 43.1 %all_to_all.30 = bf16[8,8,8,128]{3,2,1,0:T(8,128)(2,1)} all-to-all(bf16[8,8,8,128]{3,2,1,0:T(8,128)(2,1)} %pick.2), channel_id=1, replica_groups=mesh['zh'=2,'x'=4,'c'=2,'y'=4,'zf'=4,'zn'=4] {'zh','zf'}, dimensions={0} | all-to-all | bytes 262144 | tf_op jit(solution)/shard_map/all_to_all | solution.py:29
  72.2 4.6 %all-to-all-start.2 = ((bf16[16,16,8,128]{3,2,1,0:T(8,128)(2,1)}), bf16[16,16,8,128]{3,2,1,0:T(8,128)(2,1)S(1)}, u32[]{:S(2)}, u32[]{:S(2)}) async-start(bf16[16,16,8,128]{3,2,1,0:T(8,128)(2,1)} %pick.3), calls=%async_computation.2 | async-start | bytes 1048576 | tf_op jit(solution)/shard_map/all_to_all | solution.py:29
  76.8 2.5 %collective-permute-start = (bf16[128,2048]{1,0:T(8,128)(2,1)S(1)}, bf16[128,2048]{1,0:T(8,128)(2,1)S(1)}, u32[]{:S(2)}, u32[]{:S(2)}) collective-permute-start(bf16[128,2048]{1,0:T(8,128)(2,1)S(1)} %bitcast.50), channel_id=1, source_target_pairs={{0,128},{128,256},{256,384},{384,0},{1,129},{129,257},{257,385},{3... | collective-permute-start | bytes 1572872 | tf_op jit(solution)/shard_map/ppermute | solution.py:189
  79.3 3.5 %collective-permute-start.1 = (bf16[128,2048]{1,0:T(8,128)(2,1)S(1)}, bf16[128,2048]{1,0:T(8,128)(2,1)S(1)}, u32[]{:S(2)}, u32[]{:S(2)}) collective-permute-start(bf16[128,2048]{1,0:T(8,128)(2,1)S(1)} %bitcast.51), channel_id=1, source_target_pairs={{0,256},{128,384},{256,0},{384,128},{1,257},{129,385},{257,1},{385... | collective-permute-start | bytes 1572872 | tf_op jit(solution)/shard_map/ppermute | solution.py:189
  82.9 3.5 %collective-permute-start.2 = (bf16[128,2048]{1,0:T(8,128)(2,1)S(1)}, bf16[128,2048]{1,0:T(8,128)(2,1)S(1)}, u32[]{:S(2)}, u32[]{:S(2)}) collective-permute-start(bf16[128,2048]{1,0:T(8,128)(2,1)S(1)} %bitcast.52), channel_id=1, source_target_pairs={{0,384},{128,0},{256,128},{384,256},{1,385},{129,1},{257,129},{385... | collective-permute-start | bytes 1572872 | tf_op jit(solution)/shard_map/ppermute | solution.py:189
  86.4 17.7 %collective-permute-done = bf16[128,2048]{1,0:T(8,128)(2,1)S(1)} collective-permute-done((bf16[128,2048]{1,0:T(8,128)(2,1)S(1)}, bf16[128,2048]{1,0:T(8,128)(2,1)S(1)}, u32[]{:S(2)}, u32[]{:S(2)}) %collective-permute-start) | collective-permute-done | bytes 524320 | tf_op jit(solution)/shard_map/ppermute | solution.py:189
  104.1 2.5 %collective-permute-done.2 = bf16[128,2048]{1,0:T(8,128)(2,1)S(1)} collective-permute-done((bf16[128,2048]{1,0:T(8,128)(2,1)S(1)}, bf16[128,2048]{1,0:T(8,128)(2,1)S(1)}, u32[]{:S(2)}, u32[]{:S(2)}) %collective-permute-start.2) | collective-permute-done | bytes 524320 | tf_op jit(solution)/shard_map/ppermute | solution.py:189
  106.8 1.9 collective-permute-start.3
  114.1 3.1 %fusion.11.b_ref = f32[512,128]{1,0:T(8,128)} fusion(bf16[512,2048]{1,0:T(8,128)(2,1)} %collective-permute-done.3, bf16[2048,128]{1,0:T(8,128)(2,1)S(1)} %bitcast.39), kind=kOutput, calls=%fused_computation.49 | convolution fusion | flops 268435456 | bytes 2883584 | tf_op jit(solution)/shard_map/dot_general | solution.py:203
  117.2 2.3 turn.1
  119.4 4.1 %all-to-all-start.4 = ((bf16[8,128,128]{2,1,0:T(8,128)(2,1)}), bf16[8,128,128]{2,1,0:T(8,128)(2,1)S(1)}, u32[]{:S(2)}, u32[]{:S(2)}) async-start(bf16[8,128,128]{2,1,0:T(8,128)(2,1)} %bitcast.40), calls=%async_computation.4 | async-start | bytes 524288 | tf_op jit(solution)/shard_map/all_to_all | solution.py:29
  123.6 2.4 %collective-permute-start.6 = (bf16[1024,128]{1,0:T(8,128)(2,1)}, bf16[1024,128]{1,0:T(8,128)(2,1)S(1)}, u32[]{:S(2)}, u32[]{:S(2)}) collective-permute-start(bf16[1024,128]{1,0:T(8,128)(2,1)} %turn.1), channel_id=1, source_target_pairs={{0,64},{64,0},{1,65},{65,1},{2,66},{66,2},{3,67},{67,3},{4,68},{68... | collective-permute-start | bytes 786440 | tf_op jit(solution)/shard_map/ppermute | solution.py:173
  129.0 2.1 all-to-all-done.4
  131.1 3.5 %all-to-all-start.3 = ((bf16[8,128,256]{2,1,0:T(8,128)(2,1)}), bf16[8,128,256]{2,1,0:T(8,128)(2,1)S(1)}, u32[]{:S(2)}, u32[]{:S(2)}) async-start(bf16[8,128,256]{2,1,0:T(8,128)(2,1)} %bitcast.33), calls=%async_computation.3 | async-start | bytes 1048576 | tf_op jit(solution)/shard_map/all_to_all | solution.py:29
  137.1 7.7 %all-to-all-done.3 = bf16[8,128,256]{2,1,0:T(8,128)(2,1)S(1)} async-done(((bf16[8,128,256]{2,1,0:T(8,128)(2,1)}), bf16[8,128,256]{2,1,0:T(8,128)(2,1)S(1)}, u32[]{:S(2)}, u32[]{:S(2)}) %all-to-all-start.3) | async-done | bytes 524320 | tf_op jit(solution)/shard_map/all_to_all | solution.py:29
  145.6 5.6 %attend_own.1 = (f32[1024,256]{1,0:T(8,128)}, f32[1024,4]{1,0:T(8,128)}) custom-call(bf16[1024,256]{1,0:T(8,128)(2,1)} %bitcast.36, bf16[1024,128]{1,0:T(8,128)(2,1)} %get-tuple-element.20.k_ref, bf16[1024,128]{1,0:T(8,128)(2,1)} %get-tuple-element.19.v_ref), custom_call_target="tpu_custom_call" | custom-call | tf_op jit(solution)/shard_map/attend_own/pallas_call | solution.py:105
  151.2 41.9 %collective-permute-done.4 = bf16[1024,128]{1,0:T(8,128)(2,1)S(1)} collective-permute-done((bf16[1024,128]{1,0:T(8,128)(2,1)S(1)}, bf16[1024,128]{1,0:T(8,128)(2,1)S(1)}, u32[]{:S(2)}, u32[]{:S(2)}) %collective-permute-start.4) | collective-permute-done | bytes 262176 | tf_op jit(solution)/shard_map/ppermute | solution.py:206
  193.1 1.9 collective-permute-start.7
  195.7 7.2 %collective-permute-done.7 = bf16[1024,128]{1,0:T(8,128)(2,1)S(1)} collective-permute-done((bf16[1024,128]{1,0:T(8,128)(2,1)S(1)}, bf16[1024,128]{1,0:T(8,128)(2,1)S(1)}, u32[]{:S(2)}, u32[]{:S(2)}) %collective-permute-start.7) | collective-permute-done | bytes 262176 | tf_op jit(solution)/shard_map/ppermute | solution.py:221
  202.9 1.9 collective-permute-start.9
  207.1 7.8 %attend_more.1 = bf16[1024,256]{1,0:T(8,128)(2,1)} custom-call(s32[2]{0:T(128)} %pad_add_fusion.1.w_ref, bf16[1024,256]{1,0:T(8,128)(2,1)} %bitcast.37, bf16[1024,128]{1,0:T(8,128)(2,1)} %copy-done.3, bf16[1024,128]{1,0:T(8,128)(2,1)} %copy-done.6, f32[1024,256]{1,0:T(8,128)} %get-tuple-element.17.acc_ref, f32[1024,4]{1,0:T(8,128)} %get-tuple-element.18.st_ref), custom_call_target="tpu_custom_call" | custom-call | tf_op jit(solution)/shard_map/attend_more/pallas_call | solution.py:161
  214.9 15.2 %all_to_all.31 = bf16[8,128,256]{2,1,0:T(8,128)(2,1)S(1)} all-to-all(bf16[8,128,256]{2,1,0:T(8,128)(2,1)} %bitcast.44), channel_id=1, replica_groups=mesh['zh'=2,'x'=4,'c'=2,'y'=4,'zf'=4,'zn'=4] {'x','c'}, dimensions={0} | all-to-all | bytes 1048576 | tf_op jit(solution)/shard_map/all_to_all | solution.py:29
  (51 shorter events, 23.9 us)
Async XLA Ops:
  0.6 76.1 %copy-start.5 = (bf16[1,128,2048]{2,1,0:T(8,128)(2,1)S(1)}, bf16[1,128,2048]{2,1,0:T(8,128)(2,1)}, u32[]{:S(2)}) copy-start(bf16[1,128,2048]{2,1,0:T(8,128)(2,1)} %param.6) | copy-start | bytes 1572868
  2.4 22.5 %all-to-all-start = ((bf16[128,8,128]{2,1,0:T(8,128)(2,1)}), bf16[128,8,128]{2,1,0:T(8,128)(2,1)S(1)}, u32[]{:S(2)}, u32[]{:S(2)}) async-start(bf16[128,8,128]{2,1,0:T(8,128)(2,1)} %bitcast.3), calls=%async_computation | async-start | bytes 524288 | tf_op jit(solution)/shard_map/all_to_all | solution.py:29
  24.9 0.7 copy-start.2
  72.2 40.4 %all-to-all-start.2 = ((bf16[16,16,8,128]{3,2,1,0:T(8,128)(2,1)}), bf16[16,16,8,128]{3,2,1,0:T(8,128)(2,1)S(1)}, u32[]{:S(2)}, u32[]{:S(2)}) async-start(bf16[16,16,8,128]{3,2,1,0:T(8,128)(2,1)} %pick.3), calls=%async_computation.2 | async-start | bytes 1048576 | tf_op jit(solution)/shard_map/all_to_all | solution.py:29
  76.8 27.3 %collective-permute-start = (bf16[128,2048]{1,0:T(8,128)(2,1)S(1)}, bf16[128,2048]{1,0:T(8,128)(2,1)S(1)}, u32[]{:S(2)}, u32[]{:S(2)}) collective-permute-start(bf16[128,2048]{1,0:T(8,128)(2,1)S(1)} %bitcast.50), channel_id=1, source_target_pairs={{0,128},{128,256},{256,384},{384,0},{1,129},{129,257},{257,385},{3... | collective-permute-start | bytes 1572872 | tf_op jit(solution)/shard_map/ppermute | solution.py:189
  79.3 24.8 %collective-permute-start.1 = (bf16[128,2048]{1,0:T(8,128)(2,1)S(1)}, bf16[128,2048]{1,0:T(8,128)(2,1)S(1)}, u32[]{:S(2)}, u32[]{:S(2)}) collective-permute-start(bf16[128,2048]{1,0:T(8,128)(2,1)S(1)} %bitcast.51), channel_id=1, source_target_pairs={{0,256},{128,384},{256,0},{384,128},{1,257},{129,385},{257,1},{385... | collective-permute-start | bytes 1572872 | tf_op jit(solution)/shard_map/ppermute | solution.py:189
  82.9 23.7 %collective-permute-start.2 = (bf16[128,2048]{1,0:T(8,128)(2,1)S(1)}, bf16[128,2048]{1,0:T(8,128)(2,1)S(1)}, u32[]{:S(2)}, u32[]{:S(2)}) collective-permute-start(bf16[128,2048]{1,0:T(8,128)(2,1)S(1)} %bitcast.52), channel_id=1, source_target_pairs={{0,384},{128,0},{256,128},{384,256},{1,385},{129,1},{257,129},{385... | collective-permute-start | bytes 1572872 | tf_op jit(solution)/shard_map/ppermute | solution.py:189
  106.8 7.4 %collective-permute-start.3 = (bf16[512,2048]{1,0:T(8,128)(2,1)S(1)}, bf16[512,2048]{1,0:T(8,128)(2,1)}, u32[]{:S(2)}, u32[]{:S(2)}) collective-permute-start(bf16[512,2048]{1,0:T(8,128)(2,1)S(1)} %pad_maximum_fusion), channel_id=1, source_target_pairs={{0,64},{64,0},{1,65},{65,1},{2,66},{66,2},{3,67},{67,3},{4,68},{68... | collective-permute-start | bytes 6291464 | tf_op jit(solution)/shard_map/ppermute | solution.py:173
  114.1 11.9 %copy-start.4 = (bf16[1,128,2048]{2,1,0:T(8,128)(2,1)S(1)}, bf16[1,128,2048]{2,1,0:T(8,128)(2,1)}, u32[]{:S(2)}) copy-start(bf16[1,128,2048]{2,1,0:T(8,128)(2,1)} %param.5) | copy-start | bytes 1572868
  119.4 7.6 %copy-start.1 = (bf16[1024,128]{1,0:T(8,128)(2,1)S(1)}, bf16[1024,128]{1,0:T(8,128)(2,1)}, u32[]{:S(2)}) copy-start(bf16[1024,128]{1,0:T(8,128)(2,1)} %turn.1) | copy-start | bytes 786436
  119.4 11.6 %all-to-all-start.4 = ((bf16[8,128,128]{2,1,0:T(8,128)(2,1)}), bf16[8,128,128]{2,1,0:T(8,128)(2,1)S(1)}, u32[]{:S(2)}, u32[]{:S(2)}) async-start(bf16[8,128,128]{2,1,0:T(8,128)(2,1)} %bitcast.40), calls=%async_computation.4 | async-start | bytes 524288 | tf_op jit(solution)/shard_map/all_to_all | solution.py:29
  123.6 12.7 %collective-permute-start.6 = (bf16[1024,128]{1,0:T(8,128)(2,1)}, bf16[1024,128]{1,0:T(8,128)(2,1)S(1)}, u32[]{:S(2)}, u32[]{:S(2)}) collective-permute-start(bf16[1024,128]{1,0:T(8,128)(2,1)} %turn.1), channel_id=1, source_target_pairs={{0,64},{64,0},{1,65},{65,1},{2,66},{66,2},{3,67},{67,3},{4,68},{68... | collective-permute-start | bytes 786440 | tf_op jit(solution)/shard_map/ppermute | solution.py:173
  127.0 66.1 %collective-permute-start.4 = (bf16[1024,128]{1,0:T(8,128)(2,1)S(1)}, bf16[1024,128]{1,0:T(8,128)(2,1)S(1)}, u32[]{:S(2)}, u32[]{:S(2)}) collective-permute-start(bf16[1024,128]{1,0:T(8,128)(2,1)S(1)} %copy-done.1), channel_id=1, source_target_pairs={{8,519},{9,520},{10,521},{11,522},{12,523},{13,524},{14,525},{15,5... | collective-permute-start | bytes 786440 | tf_op jit(solution)/shard_map/ppermute | solution.py:206
  128.3 64.8 %collective-permute-start.5 = (bf16[1024,128]{1,0:T(8,128)(2,1)S(1)}, bf16[1024,128]{1,0:T(8,128)(2,1)S(1)}, u32[]{:S(2)}, u32[]{:S(2)}) collective-permute-start(bf16[1024,128]{1,0:T(8,128)(2,1)S(1)} %copy-done.1), channel_id=1, source_target_pairs={{0,513},{1,514},{2,515},{3,516},{4,517},{5,518},{6,519},{7,520},{1... | collective-permute-start | bytes 786440 | tf_op jit(solution)/shard_map/ppermute | solution.py:207
  131.1 13.7 %all-to-all-start.3 = ((bf16[8,128,256]{2,1,0:T(8,128)(2,1)}), bf16[8,128,256]{2,1,0:T(8,128)(2,1)S(1)}, u32[]{:S(2)}, u32[]{:S(2)}) async-start(bf16[8,128,256]{2,1,0:T(8,128)(2,1)} %bitcast.33), calls=%async_computation.3 | async-start | bytes 1048576 | tf_op jit(solution)/shard_map/all_to_all | solution.py:29
  144.8 0.8 copy-start
  193.1 9.8 %collective-permute-start.7 = (bf16[1024,128]{1,0:T(8,128)(2,1)S(1)}, bf16[1024,128]{1,0:T(8,128)(2,1)S(1)}, u32[]{:S(2)}, u32[]{:S(2)}) collective-permute-start(bf16[1024,128]{1,0:T(8,128)(2,1)S(1)} %collective-permute-done.4), channel_id=1, source_target_pairs={{519,520},{520,521},{521,522},{522,523},{523,524},{524,525},{525,5... | collective-permute-start | bytes 786440 | tf_op jit(solution)/shard_map/ppermute | solution.py:221
  195.0 7.9 %collective-permute-start.8 = (bf16[1024,128]{1,0:T(8,128)(2,1)S(1)}, bf16[1024,128]{1,0:T(8,128)(2,1)S(1)}, u32[]{:S(2)}, u32[]{:S(2)}) collective-permute-start(bf16[1024,128]{1,0:T(8,128)(2,1)S(1)} %collective-permute-done.5), channel_id=1, source_target_pairs={{513,512},{514,513},{515,514},{516,515},{517,516},{518,517},{519,5... | collective-permute-start | bytes 786440 | tf_op jit(solution)/shard_map/ppermute | solution.py:222
  202.9 3.4 %copy-start.3 = (bf16[1024,128]{1,0:T(8,128)(2,1)}, bf16[1024,128]{1,0:T(8,128)(2,1)S(1)}, u32[]{:S(2)}) copy-start(bf16[1024,128]{1,0:T(8,128)(2,1)S(1)} %broadcast_select_fusion.a_ref) | copy-start | bytes 786436
  202.9 3.4 %collective-permute-start.9 = (bf16[1024,128]{1,0:T(8,128)(2,1)S(1)}, bf16[1024,128]{1,0:T(8,128)(2,1)S(1)}, u32[]{:S(2)}, u32[]{:S(2)}) collective-permute-start(bf16[1024,128]{1,0:T(8,128)(2,1)S(1)} %broadcast_select_fusion.a_ref), channel_id=1, source_target_pairs={{0,64},{64,0},{1,65},{65,1},{2,66},{66,2},{3,67},{67,3},{4,68},{68... | collective-permute-start | bytes 786440 | tf_op jit(solution)/shard_map/ppermute | solution.py:173
  206.4 0.7 copy-start.6

commit v3 on v2

--- a/solution.py
+++ b/solution.py
@@ -175,7 +175,6 @@
 
 def layer(queries, normed, key_weight_copies, value_weight_copies, owner):
     zh, x, c = lax.axis_index("zh"), lax.axis_index("x"), lax.axis_index("c")
-    z_lo = lax.axis_index(("zf", "zn"))
     own_y, own_zf, own_zn = owner // 16, (owner // 4) % 4, owner % 4
     block8 = jnp.arange(8, dtype=jnp.int32)
     n = normed[0]
@@ -203,8 +202,7 @@
     raw = [jnp.dot(r, w, preferred_element_type=jnp.float32) for r in (mine, other)]
     kv = turn(place, *raw, cos, sin)
 
-    up = lax.ppermute(kv, RING, [(i, i + 15) for i in range(8, 16)])
-    down = lax.ppermute(kv, RING, [(i, i + 17) for i in range(8)])
+    first = lax.ppermute(kv, RING, [(i, i + 16) for i in range(16)])
 
     partner = swap_cores(kv)
     keys, values = jnp.where(c == 0, kv, partner), jnp.where(c == 0, partner, kv)
@@ -215,12 +213,9 @@
     cache_keys = cache[:, 0].transpose(1, 0, 2).reshape(1, 128, 512)
     cache_values = cache[:, 1].transpose(1, 0, 2).reshape(1, 128, 512)
 
-    up, down, state, cache_keys, cache_values = lax.optimization_barrier(
-        (up, down, state, cache_keys, cache_values)
+    first, state, cache_keys, cache_values = lax.optimization_barrier(
+        (first, state, cache_keys, cache_values)
     )
-    up = lax.ppermute(up, RING, [(i, i + 1) for i in range(23, 31)])
-    down = lax.ppermute(down, RING, [(i, i - 1) for i in range(17, 25)])
-    first = jnp.where(z_lo >= 8, up, down)
     partner = swap_cores(first)
     state = attend_more(jnp.stack([zh, c]), q, first, partner, *state)
     out = exchange(state.reshape(8, 128, 256), ("x", "c"))

time: 232 us -> 224 us (0.966)
  the two profiles are of different devices: /device:TPU:960 before, /device:TPU:968 now
where the time goes in v3:
time: 224 us; the launch traced here: 223 us
  waiting for transfers between devices  83.6 us (37%)
  blocking collectives  58.2 us (26%)
  starting transfers between devices  41.1 us (18%)
  Pallas kernels  19.1 us (9%)
  other arithmetic  8.38 us (4%)
  local copies, waits for them, and re-layouts  7.08 us (3%)
  matrix products  4.48 us (2%)
    all_to_all x2, blocking collectives, exchange(): return lax.all_to_all(x, axes, 0, 0, tiled=True)  58.2 us
    ppermute x1, waiting for transfers between devices, layer(): first = lax.ppermute(kv, RING, [(i, i + 16) for i in range(16)])  43.3 us
    all_to_all x4, starting transfers between devices, exchange(): return lax.all_to_all(x, axes, 0, 0, tiled=True)  24.1 us
    ppermute x3, waiting for transfers between devices, layer(): rows.append(lax.ppermute(n, 'x', [(i, (i + s) % 4) for i in range(4)]))  20.2 us
    all_to_all x4, waiting for transfers between devices, exchange(): return lax.all_to_all(x, axes, 0, 0, tiled=True)  19.2 us
    ppermute x3, starting transfers between devices, layer(): rows.append(lax.ppermute(n, 'x', [(i, (i + s) % 4) for i in range(4)]))  9.55 us
    pallas_call x1, Pallas kernels, attend_more(): pl.pallas_call(kernel, grid=(1024 // QB,), out_shape=jax.ShapeDtypeStruct...  7.8 us
    ppermute x3, starting transfers between devices, swap_cores(): return lax.ppermute(x, 'c', [(0, 1), (1, 0)])  6.24 us
  transfers between devices with their start and end apart: 11, of which 7 were waited for; matrix products, arithmetic and copies ran while one was open for 5% of the time, Pallas kernels for 3%

profile of v3, /device:TPU:968, one launch (start us, length us, event | category | flops | bytes accessed | tf_op | source)
XLA Modules:
  0.0 222.9 jit_solution(15257320802782948078)
XLA Ops:
  2.4 11.0 %all-to-all-start = ((bf16[128,8,128]{2,1,0:T(8,128)(2,1)}), bf16[128,8,128]{2,1,0:T(8,128)(2,1)S(1)}, u32[]{:S(2)}, u32[]{:S(2)}) async-start(bf16[128,8,128]{2,1,0:T(8,128)(2,1)} %bitcast.3), calls=%async_computation | async-start | bytes 524288 | tf_op jit(solution)/shard_map/all_to_all | solution.py:29
  15.3 8.7 %all-to-all-done.x_ref = bf16[128,8,128]{2,1,0:T(8,128)(2,1)S(1)} async-done(((bf16[128,8,128]{2,1,0:T(8,128)(2,1)}), bf16[128,8,128]{2,1,0:T(8,128)(2,1)S(1)}, u32[]{:S(2)}, u32[]{:S(2)}) %all-to-all-start) | async-done | bytes 262176 | tf_op jit(solution)/shard_map/all_to_all | solution.py:29
  26.3 43.1 %all_to_all.30 = bf16[8,8,8,128]{3,2,1,0:T(8,128)(2,1)} all-to-all(bf16[8,8,8,128]{3,2,1,0:T(8,128)(2,1)} %pick.2), channel_id=1, replica_groups=mesh['zh'=2,'x'=4,'c'=2,'y'=4,'zf'=4,'zn'=4] {'zh','zf'}, dimensions={0} | all-to-all | bytes 262144 | tf_op jit(solution)/shard_map/all_to_all | solution.py:29
  69.4 1.8 pick.3
  71.2 5.5 %all-to-all-start.2 = ((bf16[16,16,8,128]{3,2,1,0:T(8,128)(2,1)}), bf16[16,16,8,128]{3,2,1,0:T(8,128)(2,1)S(1)}, u32[]{:S(2)}, u32[]{:S(2)}) async-start(bf16[16,16,8,128]{3,2,1,0:T(8,128)(2,1)} %pick.3), calls=%async_computation.2 | async-start | bytes 1048576 | tf_op jit(solution)/shard_map/all_to_all | solution.py:29
  76.7 2.5 %collective-permute-start = (bf16[128,2048]{1,0:T(8,128)(2,1)S(1)}, bf16[128,2048]{1,0:T(8,128)(2,1)S(1)}, u32[]{:S(2)}, u32[]{:S(2)}) collective-permute-start(bf16[128,2048]{1,0:T(8,128)(2,1)S(1)} %bitcast.50), channel_id=1, source_target_pairs={{0,128},{128,256},{256,384},{384,0},{1,129},{129,257},{257,385},{3... | collective-permute-start | bytes 1572872 | tf_op jit(solution)/shard_map/ppermute | solution.py:188
  79.2 3.5 %collective-permute-start.1 = (bf16[128,2048]{1,0:T(8,128)(2,1)S(1)}, bf16[128,2048]{1,0:T(8,128)(2,1)S(1)}, u32[]{:S(2)}, u32[]{:S(2)}) collective-permute-start(bf16[128,2048]{1,0:T(8,128)(2,1)S(1)} %bitcast.51), channel_id=1, source_target_pairs={{0,256},{128,384},{256,0},{384,128},{1,257},{129,385},{257,1},{385... | collective-permute-start | bytes 1572872 | tf_op jit(solution)/shard_map/ppermute | solution.py:188
  82.7 3.5 %collective-permute-start.2 = (bf16[128,2048]{1,0:T(8,128)(2,1)S(1)}, bf16[128,2048]{1,0:T(8,128)(2,1)S(1)}, u32[]{:S(2)}, u32[]{:S(2)}) collective-permute-start(bf16[128,2048]{1,0:T(8,128)(2,1)S(1)} %bitcast.52), channel_id=1, source_target_pairs={{0,384},{128,0},{256,128},{384,256},{1,385},{129,1},{257,129},{385... | collective-permute-start | bytes 1572872 | tf_op jit(solution)/shard_map/ppermute | solution.py:188
  86.2 17.7 %collective-permute-done = bf16[128,2048]{1,0:T(8,128)(2,1)S(1)} collective-permute-done((bf16[128,2048]{1,0:T(8,128)(2,1)S(1)}, bf16[128,2048]{1,0:T(8,128)(2,1)S(1)}, u32[]{:S(2)}, u32[]{:S(2)}) %collective-permute-start) | collective-permute-done | bytes 524320 | tf_op jit(solution)/shard_map/ppermute | solution.py:188
  104.0 2.5 %collective-permute-done.2 = bf16[128,2048]{1,0:T(8,128)(2,1)S(1)} collective-permute-done((bf16[128,2048]{1,0:T(8,128)(2,1)S(1)}, bf16[128,2048]{1,0:T(8,128)(2,1)S(1)}, u32[]{:S(2)}, u32[]{:S(2)}) %collective-permute-start.2) | collective-permute-done | bytes 524320 | tf_op jit(solution)/shard_map/ppermute | solution.py:188
  106.6 1.9 collective-permute-start.3
  109.2 1.9 fusion
  114.0 3.1 %fusion.11.b_ref = f32[512,128]{1,0:T(8,128)} fusion(bf16[512,2048]{1,0:T(8,128)(2,1)} %collective-permute-done.3, bf16[2048,128]{1,0:T(8,128)(2,1)S(1)} %bitcast.39), kind=kOutput, calls=%fused_computation.48 | convolution fusion | flops 268435456 | bytes 2883584 | tf_op jit(solution)/shard_map/dot_general | solution.py:202
  117.1 2.3 %turn.1 = bf16[1024,128]{1,0:T(8,128)(2,1)} custom-call(s32[8]{0:T(128)} %pad_add_fusion.p_ref, f32[512,128]{1,0:T(8,128)} %fusion.10.a_ref, f32[512,128]{1,0:T(8,128)} %fusion.11.b_ref, f32[1024,128]{1,0:T(8,128)} %get-tuple-element.28.cos_ref, f32[1024,128]{1,0:T(8,128)} %get-tuple-element.29.sin_ref), custom_call_target="tpu_custom_call" | custom-call | tf_op jit(solution)/shard_map/turn/pallas_call | solution.py:73
  119.4 4.1 %all-to-all-start.4 = ((bf16[8,128,128]{2,1,0:T(8,128)(2,1)}), bf16[8,128,128]{2,1,0:T(8,128)(2,1)S(1)}, u32[]{:S(2)}, u32[]{:S(2)}) async-start(bf16[8,128,128]{2,1,0:T(8,128)(2,1)} %bitcast.40), calls=%async_computation.4 | async-start | bytes 524288 | tf_op jit(solution)/shard_map/all_to_all | solution.py:29
  123.5 2.4 %collective-permute-start.5 = (bf16[1024,128]{1,0:T(8,128)(2,1)}, bf16[1024,128]{1,0:T(8,128)(2,1)S(1)}, u32[]{:S(2)}, u32[]{:S(2)}) collective-permute-start(bf16[1024,128]{1,0:T(8,128)(2,1)} %turn.1), channel_id=1, source_target_pairs={{0,64},{64,0},{1,65},{65,1},{2,66},{66,2},{3,67},{67,3},{4,68},{68... | collective-permute-start | bytes 786440 | tf_op jit(solution)/shard_map/ppermute | solution.py:173
  128.2 2.8 %all-to-all-done.4 = bf16[8,128,128]{2,1,0:T(8,128)(2,1)S(1)} async-done(((bf16[8,128,128]{2,1,0:T(8,128)(2,1)}), bf16[8,128,128]{2,1,0:T(8,128)(2,1)S(1)}, u32[]{:S(2)}, u32[]{:S(2)}) %all-to-all-start.4) | async-done | bytes 262176 | tf_op jit(solution)/shard_map/all_to_all | solution.py:29
  131.0 3.5 %all-to-all-start.3 = ((bf16[8,128,256]{2,1,0:T(8,128)(2,1)}), bf16[8,128,256]{2,1,0:T(8,128)(2,1)S(1)}, u32[]{:S(2)}, u32[]{:S(2)}) async-start(bf16[8,128,256]{2,1,0:T(8,128)(2,1)} %bitcast.33), calls=%async_computation.3 | async-start | bytes 1048576 | tf_op jit(solution)/shard_map/all_to_all | solution.py:29
  137.0 7.7 %all-to-all-done.3 = bf16[8,128,256]{2,1,0:T(8,128)(2,1)S(1)} async-done(((bf16[8,128,256]{2,1,0:T(8,128)(2,1)}), bf16[8,128,256]{2,1,0:T(8,128)(2,1)S(1)}, u32[]{:S(2)}, u32[]{:S(2)}) %all-to-all-start.3) | async-done | bytes 524320 | tf_op jit(solution)/shard_map/all_to_all | solution.py:29
  145.5 5.6 %attend_own.1 = (f32[1024,256]{1,0:T(8,128)}, f32[1024,4]{1,0:T(8,128)}) custom-call(bf16[1024,256]{1,0:T(8,128)(2,1)} %bitcast.36, bf16[1024,128]{1,0:T(8,128)(2,1)} %get-tuple-element.18.k_ref, bf16[1024,128]{1,0:T(8,128)(2,1)} %get-tuple-element.17.v_ref), custom_call_target="tpu_custom_call" | custom-call | tf_op jit(solution)/shard_map/attend_own/pallas_call | solution.py:105
  151.2 43.3 %collective-permute-done.4.a_ref = bf16[1024,128]{1,0:T(8,128)(2,1)S(1)} collective-permute-done((bf16[1024,128]{1,0:T(8,128)(2,1)S(1)}, bf16[1024,128]{1,0:T(8,128)(2,1)S(1)}, u32[]{:S(2)}, u32[]{:S(2)}) %collective-permute-start.4) | collective-permute-done | bytes 262176 | tf_op jit(solution)/shard_map/ppermute | solution.py:205
  194.5 1.9 collective-permute-start.6
  198.6 7.8 %attend_more.1 = bf16[1024,256]{1,0:T(8,128)(2,1)} custom-call(s32[2]{0:T(128)} %pad_add_fusion.1.w_ref, bf16[1024,256]{1,0:T(8,128)(2,1)} %bitcast.37, bf16[1024,128]{1,0:T(8,128)(2,1)} %copy-done.5, bf16[1024,128]{1,0:T(8,128)(2,1)} %copy-done.6, f32[1024,256]{1,0:T(8,128)} %get-tuple-element.15.acc_ref, f32[1024,4]{1,0:T(8,128)} %get-tuple-element.16.st_ref), custom_call_target="tpu_custom_call" | custom-call | tf_op jit(solution)/shard_map/attend_more/pallas_call | solution.py:161
  206.4 15.1 %all_to_all.31 = bf16[8,128,256]{2,1,0:T(8,128)(2,1)S(1)} all-to-all(bf16[8,128,256]{2,1,0:T(8,128)(2,1)} %bitcast.44), channel_id=1, replica_groups=mesh['zh'=2,'x'=4,'c'=2,'y'=4,'zf'=4,'zn'=4] {'x','c'}, dimensions={0} | all-to-all | bytes 1048576 | tf_op jit(solution)/shard_map/all_to_all | solution.py:29
  (44 shorter events, 18.7 us)
Async XLA Ops:
  0.6 76.0 %copy-start.4 = (bf16[1,128,2048]{2,1,0:T(8,128)(2,1)S(1)}, bf16[1,128,2048]{2,1,0:T(8,128)(2,1)}, u32[]{:S(2)}) copy-start(bf16[1,128,2048]{2,1,0:T(8,128)(2,1)} %param.6) | copy-start | bytes 1572868
  2.4 21.5 %all-to-all-start = ((bf16[128,8,128]{2,1,0:T(8,128)(2,1)}), bf16[128,8,128]{2,1,0:T(8,128)(2,1)S(1)}, u32[]{:S(2)}, u32[]{:S(2)}) async-start(bf16[128,8,128]{2,1,0:T(8,128)(2,1)} %bitcast.3), calls=%async_computation | async-start | bytes 524288 | tf_op jit(solution)/shard_map/all_to_all | solution.py:29
  24.0 0.7 copy-start.2
  71.2 41.2 %all-to-all-start.2 = ((bf16[16,16,8,128]{3,2,1,0:T(8,128)(2,1)}), bf16[16,16,8,128]{3,2,1,0:T(8,128)(2,1)S(1)}, u32[]{:S(2)}, u32[]{:S(2)}) async-start(bf16[16,16,8,128]{3,2,1,0:T(8,128)(2,1)} %pick.3), calls=%async_computation.2 | async-start | bytes 1048576 | tf_op jit(solution)/shard_map/all_to_all | solution.py:29
  76.7 27.3 %collective-permute-start = (bf16[128,2048]{1,0:T(8,128)(2,1)S(1)}, bf16[128,2048]{1,0:T(8,128)(2,1)S(1)}, u32[]{:S(2)}, u32[]{:S(2)}) collective-permute-start(bf16[128,2048]{1,0:T(8,128)(2,1)S(1)} %bitcast.50), channel_id=1, source_target_pairs={{0,128},{128,256},{256,384},{384,0},{1,129},{129,257},{257,385},{3... | collective-permute-start | bytes 1572872 | tf_op jit(solution)/shard_map/ppermute | solution.py:188
  79.2 24.8 %collective-permute-start.1 = (bf16[128,2048]{1,0:T(8,128)(2,1)S(1)}, bf16[128,2048]{1,0:T(8,128)(2,1)S(1)}, u32[]{:S(2)}, u32[]{:S(2)}) collective-permute-start(bf16[128,2048]{1,0:T(8,128)(2,1)S(1)} %bitcast.51), channel_id=1, source_target_pairs={{0,256},{128,384},{256,0},{384,128},{1,257},{129,385},{257,1},{385... | collective-permute-start | bytes 1572872 | tf_op jit(solution)/shard_map/ppermute | solution.py:188
  82.7 23.7 %collective-permute-start.2 = (bf16[128,2048]{1,0:T(8,128)(2,1)S(1)}, bf16[128,2048]{1,0:T(8,128)(2,1)S(1)}, u32[]{:S(2)}, u32[]{:S(2)}) collective-permute-start(bf16[128,2048]{1,0:T(8,128)(2,1)S(1)} %bitcast.52), channel_id=1, source_target_pairs={{0,384},{128,0},{256,128},{384,256},{1,385},{129,1},{257,129},{385... | collective-permute-start | bytes 1572872 | tf_op jit(solution)/shard_map/ppermute | solution.py:188
  106.6 7.4 %collective-permute-start.3 = (bf16[512,2048]{1,0:T(8,128)(2,1)S(1)}, bf16[512,2048]{1,0:T(8,128)(2,1)}, u32[]{:S(2)}, u32[]{:S(2)}) collective-permute-start(bf16[512,2048]{1,0:T(8,128)(2,1)S(1)} %pad_maximum_fusion), channel_id=1, source_target_pairs={{0,64},{64,0},{1,65},{65,1},{2,66},{66,2},{3,67},{67,3},{4,68},{68... | collective-permute-start | bytes 6291464 | tf_op jit(solution)/shard_map/ppermute | solution.py:173
  114.0 11.9 %copy-start.3 = (bf16[1,128,2048]{2,1,0:T(8,128)(2,1)S(1)}, bf16[1,128,2048]{2,1,0:T(8,128)(2,1)}, u32[]{:S(2)}) copy-start(bf16[1,128,2048]{2,1,0:T(8,128)(2,1)} %param.5) | copy-start | bytes 1572868
  119.4 7.6 %copy-start.1 = (bf16[1024,128]{1,0:T(8,128)(2,1)S(1)}, bf16[1024,128]{1,0:T(8,128)(2,1)}, u32[]{:S(2)}) copy-start(bf16[1024,128]{1,0:T(8,128)(2,1)} %turn.1) | copy-start | bytes 786436
  119.4 11.6 %all-to-all-start.4 = ((bf16[8,128,128]{2,1,0:T(8,128)(2,1)}), bf16[8,128,128]{2,1,0:T(8,128)(2,1)S(1)}, u32[]{:S(2)}, u32[]{:S(2)}) async-start(bf16[8,128,128]{2,1,0:T(8,128)(2,1)} %bitcast.40), calls=%async_computation.4 | async-start | bytes 524288 | tf_op jit(solution)/shard_map/all_to_all | solution.py:29
  123.5 12.7 %collective-permute-start.5 = (bf16[1024,128]{1,0:T(8,128)(2,1)}, bf16[1024,128]{1,0:T(8,128)(2,1)S(1)}, u32[]{:S(2)}, u32[]{:S(2)}) collective-permute-start(bf16[1024,128]{1,0:T(8,128)(2,1)} %turn.1), channel_id=1, source_target_pairs={{0,64},{64,0},{1,65},{65,1},{2,66},{66,2},{3,67},{67,3},{4,68},{68... | collective-permute-start | bytes 786440 | tf_op jit(solution)/shard_map/ppermute | solution.py:173
  126.9 67.6 %collective-permute-start.4 = (bf16[1024,128]{1,0:T(8,128)(2,1)S(1)}, bf16[1024,128]{1,0:T(8,128)(2,1)S(1)}, u32[]{:S(2)}, u32[]{:S(2)}) collective-permute-start(bf16[1024,128]{1,0:T(8,128)(2,1)S(1)} %copy-done.1), channel_id=1, source_target_pairs={{0,512},{1,513},{2,514},{3,515},{4,516},{5,517},{6,518},{7,519},{8... | collective-permute-start | bytes 786440 | tf_op jit(solution)/shard_map/ppermute | solution.py:205
  131.0 13.7 %all-to-all-start.3 = ((bf16[8,128,256]{2,1,0:T(8,128)(2,1)}), bf16[8,128,256]{2,1,0:T(8,128)(2,1)S(1)}, u32[]{:S(2)}, u32[]{:S(2)}) async-start(bf16[8,128,256]{2,1,0:T(8,128)(2,1)} %bitcast.33), calls=%async_computation.3 | async-start | bytes 1048576 | tf_op jit(solution)/shard_map/all_to_all | solution.py:29
  144.7 0.8 copy-start
  194.5 3.4 %copy-start.5 = (bf16[1024,128]{1,0:T(8,128)(2,1)}, bf16[1024,128]{1,0:T(8,128)(2,1)S(1)}, u32[]{:S(2)}) copy-start(bf16[1024,128]{1,0:T(8,128)(2,1)S(1)} %collective-permute-done.4.a_ref) | copy-start | bytes 786436
  194.5 3.4 %collective-permute-start.6 = (bf16[1024,128]{1,0:T(8,128)(2,1)S(1)}, bf16[1024,128]{1,0:T(8,128)(2,1)S(1)}, u32[]{:S(2)}, u32[]{:S(2)}) collective-permute-start(bf16[1024,128]{1,0:T(8,128)(2,1)S(1)} %collective-permute-done.4.a_ref), channel_id=1, source_target_pairs={{0,64},{64,0},{1,65},{65,1},{2,66},{66,2},{3,67},{67,3},{4,68},{68... | collective-permute-start | bytes 786440 | tf_op jit(solution)/shard_map/ppermute | solution.py:173
  197.9 0.7 copy-start.6

commit v4 on v3

--- a/solution.py
+++ b/solution.py
@@ -62,21 +62,51 @@
     return jnp.where(is_key, cos, 1.0), jnp.where(is_key, sin, 0.0)
 
 
-def turn(place, mine, other, cos, sin):
-    def kernel(p_ref, a_ref, b_ref, cos_ref, sin_ref, o_ref):
-        for k in range(8):
-            part = (a_ref if k < 4 else b_ref)[pl.ds(128 * (k % 4), 128), :]
-            to = pl.ds(pl.multiple_of(p_ref[k] * 128, 128), 128)
-            turned = part * cos_ref[to, :] + pltpu.roll(part, 64, 1) * sin_ref[to, :]
-            o_ref[to, :] = turned.astype(jnp.bfloat16)
-
+def project(run, place, mine, other, w, cos, sin, before=None):
+    def kernel(p_ref, a0, a1, a2, a3, b_ref, w_ref, cos_ref, sin_ref, *rest):
+        old, (o_ref, rows, wv, cv, sv, sems) = rest[:-6], rest[-6:]
+
+        @pl.when(p_ref[8] == 1)
+        def _():
+            pairs = [(w_ref, wv), (cos_ref, cv), (sin_ref, sv)]
+            pairs += [(a, rows.at[k]) for k, a in enumerate((a0, a1, a2, a3))]
+            pairs += [(b_ref.at[pl.ds(128 * k, 128)], rows.at[4 + k]) for k in range(4)]
+            copies = [pltpu.make_async_copy(s, d, sems.at[k]) for k, (s, d) in enumerate(pairs)]
+            for copy in copies:
+                copy.start()
+            for copy in copies[:3]:
+                copy.wait()
+            for k in range(8):
+                copies[3 + k].wait()
+                raw = jnp.dot(rows[k], wv[...], preferred_element_type=jnp.float32)
+                to = pl.ds(pl.multiple_of(p_ref[k] * 128, 128), 128)
+                turned = raw * cv[to, :] + pltpu.roll(raw, 64, 1) * sv[to, :]
+                o_ref[to, :] = turned.astype(jnp.bfloat16)
+
+        @pl.when(p_ref[8] != 1)
+        def _():
+            if old:
+                copy = pltpu.make_async_copy(old[0], o_ref, sems.at[0])
+                copy.start()
+                copy.wait()
+            else:
+                o_ref[...] = jnp.zeros_like(o_ref)
+
+    extra = () if before is None else (before,)
     return pl.pallas_call(
         kernel,
         out_shape=jax.ShapeDtypeStruct((1024, HEAD), jnp.bfloat16),
-        in_specs=[SM] + [VM] * 4,
+        in_specs=[SM] + [pl.BlockSpec(memory_space=pl.ANY)] * (8 + len(extra)),
         out_specs=VM,
-        name="turn",
-    )(place, mine, other, cos, sin)
+        scratch_shapes=[
+            pltpu.VMEM((8, 128, 2048), jnp.bfloat16),
+            pltpu.VMEM((2048, HEAD), jnp.bfloat16),
+            pltpu.VMEM((1024, HEAD), jnp.float32),
+            pltpu.VMEM((1024, HEAD), jnp.float32),
+            pltpu.SemaphoreType.DMA((11,)),
+        ],
+        name="project",
+    )(jnp.concatenate([place, run.reshape(1)]), *mine, other, w, cos, sin, *extra)
 
 
 def attend_own(q, k, v):
@@ -193,17 +223,18 @@
     w = pick_spread(w.reshape(64, 8, HEAD), index, 16, ("y", "zn"))
     w = w.transpose(1, 0, 2, 3).reshape(2048, HEAD)
 
-    mine = jnp.concatenate(rows)
-    other = swap_cores(mine)
+    other = swap_cores(jnp.concatenate(rows))
 
     chip = (x - jnp.arange(4, dtype=jnp.int32)) % 4
     place = jnp.concatenate([chip * 2 + c, chip * 2 + 1 - c])
-    cos, sin = tables(zh, c)
-    raw = [jnp.dot(r, w, preferred_element_type=jnp.float32) for r in (mine, other)]
-    kv = turn(place, *raw, cos, sin)
-
-    first = lax.ppermute(kv, RING, [(i, i + 16) for i in range(16)])
-
+    other, half = lax.optimization_barrier((other, zh))
+    cos, sin = tables(half, c)
+    parts = (place, rows, other, w, cos, sin)
+
+    sent = project(1 - zh, *parts)
+    first = lax.ppermute(sent, RING, [(i, i + 16) for i in range(16)])
+
+    kv = project(zh, *parts, sent)
     partner = swap_cores(kv)
     keys, values = jnp.where(c == 0, kv, partner), jnp.where(c == 0, partner, kv)
     q = queries[0].reshape(128, 8, 256).transpose(1, 0, 2)

time: 224 us -> 231 us (1.031)
  Pallas kernels: 19.1 us -> 24.3 us
  matrix products: 4.48 us -> 0 us
  waiting for transfers between devices: 83.6 us -> 87.2 us
    pallas_call x1 -> x2, Pallas kernels: 2.29 us -> 7.54 us  [project(): pl.pallas_call(kernel, out_shape=jax.ShapeDtypeStruct((1024, HEAD), jnp.b...]
    dot_general x2 -> x0, matrix products: 4.48 us -> none  [layer(): jnp.dot(r, w, preferred_element_type=jnp.float32)]
    ppermute x3, waiting for transfers between devices: 0.84 us -> 4.55 us  [swap_cores(): return lax.ppermute(x, 'c', [(0, 1), (1, 0)])]
  transfers between devices with their start and end apart: 11 -> 11, of which waited for: 7 -> 8; matrix products, arithmetic and copies ran while one was open for 5% -> 5% of each run, Pallas kernels for 3% -> 2%
where the time goes in v4:
time: 231 us; the launch traced here: 230 us
  waiting for transfers between devices  87.2 us (38%)
  blocking collectives  58.2 us (25%)
  starting transfers between devices  41.2 us (18%)
  Pallas kernels  24.3 us (11%)
  other arithmetic  9.74 us (4%)
  local copies, waits for them, and re-layouts  7.93 us (3%)
    all_to_all x2, blocking collectives, exchange(): return lax.all_to_all(x, axes, 0, 0, tiled=True)  58.2 us
    ppermute x1, waiting for transfers between devices, layer(): first = lax.ppermute(sent, RING, [(i, i + 16) for i in range(16)])  43.4 us
    all_to_all x4, starting transfers between devices, exchange(): return lax.all_to_all(x, axes, 0, 0, tiled=True)  24.2 us
    ppermute x3, waiting for transfers between devices, layer(): rows.append(lax.ppermute(n, 'x', [(i, (i + s) % 4) for i in range(4)]))  20.2 us
    all_to_all x4, waiting for transfers between devices, exchange(): return lax.all_to_all(x, axes, 0, 0, tiled=True)  19.1 us
    ppermute x3, starting transfers between devices, layer(): rows.append(lax.ppermute(n, 'x', [(i, (i + s) % 4) for i in range(4)]))  9.55 us
    pallas_call x1, Pallas kernels, attend_more(): pl.pallas_call(kernel, grid=(1024 // QB,), out_shape=jax.ShapeDtypeStruct...  7.79 us
    pallas_call x2, Pallas kernels, project(): pl.pallas_call(kernel, out_shape=jax.ShapeDtypeStruct((1024, HEAD), jnp.b...  7.54 us
  transfers between devices with their start and end apart: 11, of which 8 were waited for; matrix products, arithmetic and copies ran while one was open for 5% of the time, Pallas kernels for 2%

profile of v4, /device:TPU:968, one launch (start us, length us, event | category | flops | bytes accessed | tf_op | source)
XLA Modules:
  0.0 229.6 jit_solution(11574210099521788696)
XLA Ops:
  2.4 11.0 %all-to-all-start = ((bf16[128,8,128]{2,1,0:T(8,128)(2,1)}), bf16[128,8,128]{2,1,0:T(8,128)(2,1)S(1)}, u32[]{:S(2)}, u32[]{:S(2)}) async-start(bf16[128,8,128]{2,1,0:T(8,128)(2,1)} %bitcast.4), calls=%async_computation | async-start | bytes 524288 | tf_op jit(solution)/shard_map/all_to_all | solution.py:29
  15.2 8.7 %all-to-all-done.x_ref = bf16[128,8,128]{2,1,0:T(8,128)(2,1)S(1)} async-done(((bf16[128,8,128]{2,1,0:T(8,128)(2,1)}), bf16[128,8,128]{2,1,0:T(8,128)(2,1)S(1)}, u32[]{:S(2)}, u32[]{:S(2)}) %all-to-all-start) | async-done | bytes 262176 | tf_op jit(solution)/shard_map/all_to_all | solution.py:29
  26.3 43.1 %all_to_all.30 = bf16[8,8,8,128]{3,2,1,0:T(8,128)(2,1)} all-to-all(bf16[8,8,8,128]{3,2,1,0:T(8,128)(2,1)} %pick.2), channel_id=1, replica_groups=mesh['zh'=2,'x'=4,'c'=2,'y'=4,'zf'=4,'zn'=4] {'zh','zf'}, dimensions={0} | all-to-all | bytes 262144 | tf_op jit(solution)/shard_map/all_to_all | solution.py:29
  69.4 1.8 pick.3
  71.2 5.5 %all-to-all-start.2 = ((bf16[16,16,8,128]{3,2,1,0:T(8,128)(2,1)}), bf16[16,16,8,128]{3,2,1,0:T(8,128)(2,1)S(1)}, u32[]{:S(2)}, u32[]{:S(2)}) async-start(bf16[16,16,8,128]{3,2,1,0:T(8,128)(2,1)} %pick.3), calls=%async_computation.2 | async-start | bytes 1048576 | tf_op jit(solution)/shard_map/all_to_all | solution.py:29
  76.7 2.5 %collective-permute-start = (bf16[128,2048]{1,0:T(8,128)(2,1)S(1)}, bf16[128,2048]{1,0:T(8,128)(2,1)S(1)}, u32[]{:S(2)}, u32[]{:S(2)}) collective-permute-start(bf16[128,2048]{1,0:T(8,128)(2,1)S(1)} %bitcast.37), channel_id=1, source_target_pairs={{0,128},{128,256},{256,384},{384,0},{1,129},{129,257},{257,385},{3... | collective-permute-start | bytes 1572872 | tf_op jit(solution)/shard_map/ppermute | solution.py:218
  79.2 3.5 %collective-permute-start.1 = (bf16[128,2048]{1,0:T(8,128)(2,1)S(1)}, bf16[128,2048]{1,0:T(8,128)(2,1)S(1)}, u32[]{:S(2)}, u32[]{:S(2)}) collective-permute-start(bf16[128,2048]{1,0:T(8,128)(2,1)S(1)} %bitcast.38), channel_id=1, source_target_pairs={{0,256},{128,384},{256,0},{384,128},{1,257},{129,385},{257,1},{385... | collective-permute-start | bytes 1572872 | tf_op jit(solution)/shard_map/ppermute | solution.py:218
  82.7 3.5 %collective-permute-start.2 = (bf16[128,2048]{1,0:T(8,128)(2,1)S(1)}, bf16[128,2048]{1,0:T(8,128)(2,1)S(1)}, u32[]{:S(2)}, u32[]{:S(2)}) collective-permute-start(bf16[128,2048]{1,0:T(8,128)(2,1)S(1)} %bitcast.39), channel_id=1, source_target_pairs={{0,384},{128,0},{256,128},{384,256},{1,385},{129,1},{257,129},{385... | collective-permute-start | bytes 1572872 | tf_op jit(solution)/shard_map/ppermute | solution.py:218
  86.2 17.7 %collective-permute-done.a1 = bf16[128,2048]{1,0:T(8,128)(2,1)S(1)} collective-permute-done((bf16[128,2048]{1,0:T(8,128)(2,1)S(1)}, bf16[128,2048]{1,0:T(8,128)(2,1)S(1)}, u32[]{:S(2)}, u32[]{:S(2)}) %collective-permute-start) | collective-permute-done | bytes 524320 | tf_op jit(solution)/shard_map/ppermute | solution.py:218
  104.0 2.5 %collective-permute-done.2.a3 = bf16[128,2048]{1,0:T(8,128)(2,1)S(1)} collective-permute-done((bf16[128,2048]{1,0:T(8,128)(2,1)S(1)}, bf16[128,2048]{1,0:T(8,128)(2,1)S(1)}, u32[]{:S(2)}, u32[]{:S(2)}) %collective-permute-start.2) | collective-permute-done | bytes 524320 | tf_op jit(solution)/shard_map/ppermute | solution.py:218
  108.1 1.9 collective-permute-start.3
  110.7 3.7 %collective-permute-done.3.b_ref = bf16[512,2048]{1,0:T(8,128)(2,1)S(1)} collective-permute-done((bf16[512,2048]{1,0:T(8,128)(2,1)}, bf16[512,2048]{1,0:T(8,128)(2,1)S(1)}, u32[]{:S(2)}, u32[]{:S(2)}) %collective-permute-start.3) | collective-permute-done | bytes 2097184 | tf_op jit(solution)/shard_map/ppermute | solution.py:203
  114.3 1.9 fusion
  120.1 6.0 %project.3 = bf16[1024,128]{1,0:T(8,128)(2,1)} custom-call(s32[9]{0:T(128)} %get-tuple-element.28.p_ref, bf16[128,2048]{1,0:T(8,128)(2,1)} %bitcast.36, bf16[128,2048]{1,0:T(8,128)(2,1)} %copy-done.2, bf16[128,2048]{1,0:T(8,128)(2,1)} %copy-done.3, bf16[128,2048]{1,0:T(8,128)(2,1)} %copy-done.4, bf16[512,2048]{1,0:T(8,128)(2,1)} %copy-done, ...), custom_call_target="tpu_custom_call" | custom-call | tf_op jit(solution)/shard_map/project/pallas_call | solution.py:96
  126.1 4.0 %all-to-all-start.4 = ((bf16[8,128,128]{2,1,0:T(8,128)(2,1)}), bf16[8,128,128]{2,1,0:T(8,128)(2,1)S(1)}, u32[]{:S(2)}, u32[]{:S(2)}) async-start(bf16[8,128,128]{2,1,0:T(8,128)(2,1)} %bitcast.43), calls=%async_computation.4 | async-start | bytes 524288 | tf_op jit(solution)/shard_map/all_to_all | solution.py:29
  130.1 2.4 %collective-permute-start.5 = (bf16[1024,128]{1,0:T(8,128)(2,1)}, bf16[1024,128]{1,0:T(8,128)(2,1)S(1)}, u32[]{:S(2)}, u32[]{:S(2)}) collective-permute-start(bf16[1024,128]{1,0:T(8,128)(2,1)} %project.3), channel_id=1, source_target_pairs={{0,64},{64,0},{1,65},{65,1},{2,66},{66,2},{3,67},{67,3},{4,68},{68... | collective-permute-start | bytes 786440 | tf_op jit(solution)/shard_map/ppermute | solution.py:203
  134.9 2.8 %all-to-all-done.4 = bf16[8,128,128]{2,1,0:T(8,128)(2,1)S(1)} async-done(((bf16[8,128,128]{2,1,0:T(8,128)(2,1)}), bf16[8,128,128]{2,1,0:T(8,128)(2,1)S(1)}, u32[]{:S(2)}, u32[]{:S(2)}) %all-to-all-start.4) | async-done | bytes 262176 | tf_op jit(solution)/shard_map/all_to_all | solution.py:29
  137.7 3.7 %all-to-all-start.3 = ((bf16[8,128,256]{2,1,0:T(8,128)(2,1)}), bf16[8,128,256]{2,1,0:T(8,128)(2,1)S(1)}, u32[]{:S(2)}, u32[]{:S(2)}) async-start(bf16[8,128,256]{2,1,0:T(8,128)(2,1)} %bitcast.30), calls=%async_computation.3 | async-start | bytes 1048576 | tf_op jit(solution)/shard_map/all_to_all | solution.py:29
  143.8 7.6 %all-to-all-done.3 = bf16[8,128,256]{2,1,0:T(8,128)(2,1)S(1)} async-done(((bf16[8,128,256]{2,1,0:T(8,128)(2,1)}), bf16[8,128,256]{2,1,0:T(8,128)(2,1)S(1)}, u32[]{:S(2)}, u32[]{:S(2)}) %all-to-all-start.3) | async-done | bytes 524320 | tf_op jit(solution)/shard_map/all_to_all | solution.py:29
  152.2 5.6 %attend_own.1 = (f32[1024,256]{1,0:T(8,128)}, f32[1024,4]{1,0:T(8,128)}) custom-call(bf16[1024,256]{1,0:T(8,128)(2,1)} %bitcast.41, bf16[1024,128]{1,0:T(8,128)(2,1)} %get-tuple-element.22.k_ref, bf16[1024,128]{1,0:T(8,128)(2,1)} %get-tuple-element.21.v_ref), custom_call_target="tpu_custom_call" | custom-call | tf_op jit(solution)/shard_map/attend_own/pallas_call | solution.py:135
  157.8 43.4 %collective-permute-done.4.a_ref = bf16[1024,128]{1,0:T(8,128)(2,1)S(1)} collective-permute-done((bf16[1024,128]{1,0:T(8,128)(2,1)S(1)}, bf16[1024,128]{1,0:T(8,128)(2,1)S(1)}, u32[]{:S(2)}, u32[]{:S(2)}) %collective-permute-start.4) | collective-permute-done | bytes 262176 | tf_op jit(solution)/shard_map/ppermute | solution.py:235
  201.2 1.9 collective-permute-start.6
  205.3 7.8 %attend_more.1 = bf16[1024,256]{1,0:T(8,128)(2,1)} custom-call(s32[2]{0:T(128)} %pad_add_fusion.3.w_ref, bf16[1024,256]{1,0:T(8,128)(2,1)} %bitcast.42, bf16[1024,128]{1,0:T(8,128)(2,1)} %copy-done.10, bf16[1024,128]{1,0:T(8,128)(2,1)} %copy-done.11, f32[1024,256]{1,0:T(8,128)} %get-tuple-element.19.acc_ref, f32[1024,4]{1,0:T(8,128)} %get-tuple-element.20.st_ref), custom_call_target="tpu_custom_call" | custom-call | tf_op jit(solution)/shard_map/attend_more/pallas_call | solution.py:191
  213.1 15.2 %all_to_all.31 = bf16[8,128,256]{2,1,0:T(8,128)(2,1)S(1)} all-to-all(bf16[8,128,256]{2,1,0:T(8,128)(2,1)} %bitcast.47), channel_id=1, replica_groups=mesh['zh'=2,'x'=4,'c'=2,'y'=4,'zf'=4,'zn'=4] {'x','c'}, dimensions={0} | all-to-all | bytes 1048576 | tf_op jit(solution)/shard_map/all_to_all | solution.py:29
  (53 shorter events, 21.1 us)
Async XLA Ops:
  0.6 76.0 %copy-start.1 = (bf16[1,128,2048]{2,1,0:T(8,128)(2,1)S(1)}, bf16[1,128,2048]{2,1,0:T(8,128)(2,1)}, u32[]{:S(2)}) copy-start(bf16[1,128,2048]{2,1,0:T(8,128)(2,1)} %param.6) | copy-start | bytes 1572868
  2.4 21.5 %all-to-all-start = ((bf16[128,8,128]{2,1,0:T(8,128)(2,1)}), bf16[128,8,128]{2,1,0:T(8,128)(2,1)S(1)}, u32[]{:S(2)}, u32[]{:S(2)}) async-start(bf16[128,8,128]{2,1,0:T(8,128)(2,1)} %bitcast.4), calls=%async_computation | async-start | bytes 524288 | tf_op jit(solution)/shard_map/all_to_all | solution.py:29
  24.0 0.7 copy-start.8
  71.2 46.4 %all-to-all-start.2 = ((bf16[16,16,8,128]{3,2,1,0:T(8,128)(2,1)}), bf16[16,16,8,128]{3,2,1,0:T(8,128)(2,1)S(1)}, u32[]{:S(2)}, u32[]{:S(2)}) async-start(bf16[16,16,8,128]{3,2,1,0:T(8,128)(2,1)} %pick.3), calls=%async_computation.2 | async-start | bytes 1048576 | tf_op jit(solution)/shard_map/all_to_all | solution.py:29
  76.7 27.3 %collective-permute-start = (bf16[128,2048]{1,0:T(8,128)(2,1)S(1)}, bf16[128,2048]{1,0:T(8,128)(2,1)S(1)}, u32[]{:S(2)}, u32[]{:S(2)}) collective-permute-start(bf16[128,2048]{1,0:T(8,128)(2,1)S(1)} %bitcast.37), channel_id=1, source_target_pairs={{0,128},{128,256},{256,384},{384,0},{1,129},{129,257},{257,385},{3... | collective-permute-start | bytes 1572872 | tf_op jit(solution)/shard_map/ppermute | solution.py:218
  79.2 24.8 %collective-permute-start.1 = (bf16[128,2048]{1,0:T(8,128)(2,1)S(1)}, bf16[128,2048]{1,0:T(8,128)(2,1)S(1)}, u32[]{:S(2)}, u32[]{:S(2)}) collective-permute-start(bf16[128,2048]{1,0:T(8,128)(2,1)S(1)} %bitcast.38), channel_id=1, source_target_pairs={{0,256},{128,384},{256,0},{384,128},{1,257},{129,385},{257,1},{385... | collective-permute-start | bytes 1572872 | tf_op jit(solution)/shard_map/ppermute | solution.py:218
  82.7 23.7 %collective-permute-start.2 = (bf16[128,2048]{1,0:T(8,128)(2,1)S(1)}, bf16[128,2048]{1,0:T(8,128)(2,1)S(1)}, u32[]{:S(2)}, u32[]{:S(2)}) collective-permute-start(bf16[128,2048]{1,0:T(8,128)(2,1)S(1)} %bitcast.39), channel_id=1, source_target_pairs={{0,384},{128,0},{256,128},{384,256},{1,385},{129,1},{257,129},{385... | collective-permute-start | bytes 1572872 | tf_op jit(solution)/shard_map/ppermute | solution.py:218
  104.0 4.1 %copy-start.2 = (bf16[128,2048]{1,0:T(8,128)(2,1)}, bf16[128,2048]{1,0:T(8,128)(2,1)S(1)}, u32[]{:S(2)}) copy-start(bf16[128,2048]{1,0:T(8,128)(2,1)S(1)} %collective-permute-done.a1) | copy-start | bytes 1572868
  104.0 4.1 %copy-start.3 = (bf16[128,2048]{1,0:T(8,128)(2,1)}, bf16[128,2048]{1,0:T(8,128)(2,1)S(1)}, u32[]{:S(2)}) copy-start(bf16[128,2048]{1,0:T(8,128)(2,1)S(1)} %collective-permute-done.1.a2) | copy-start | bytes 1572868
  106.5 1.6 copy-start.4
  108.1 6.3 %collective-permute-start.3 = (bf16[512,2048]{1,0:T(8,128)(2,1)}, bf16[512,2048]{1,0:T(8,128)(2,1)S(1)}, u32[]{:S(2)}, u32[]{:S(2)}) collective-permute-start(bf16[512,2048]{1,0:T(8,128)(2,1)} %pad_maximum_fusion), channel_id=1, source_target_pairs={{0,64},{64,0},{1,65},{65,1},{2,66},{66,2},{3,67},{67,3},{4,68},{68... | collective-permute-start | bytes 6291464 | tf_op jit(solution)/shard_map/ppermute | solution.py:203
  114.3 3.2 %copy-start = (bf16[512,2048]{1,0:T(8,128)(2,1)}, bf16[512,2048]{1,0:T(8,128)(2,1)S(1)}, u32[]{:S(2)}) copy-start(bf16[512,2048]{1,0:T(8,128)(2,1)S(1)} %collective-permute-done.3.b_ref) | copy-start | bytes 6291460
  120.0 12.5 %copy-start.9 = (bf16[1,128,2048]{2,1,0:T(8,128)(2,1)S(1)}, bf16[1,128,2048]{2,1,0:T(8,128)(2,1)}, u32[]{:S(2)}) copy-start(bf16[1,128,2048]{2,1,0:T(8,128)(2,1)} %param.5) | copy-start | bytes 1572868
  126.1 7.5 %copy-start.7 = (bf16[1024,128]{1,0:T(8,128)(2,1)S(1)}, bf16[1024,128]{1,0:T(8,128)(2,1)}, u32[]{:S(2)}) copy-start(bf16[1024,128]{1,0:T(8,128)(2,1)} %project.2.rest_0_) | copy-start | bytes 786436
  126.1 11.6 %all-to-all-start.4 = ((bf16[8,128,128]{2,1,0:T(8,128)(2,1)}), bf16[8,128,128]{2,1,0:T(8,128)(2,1)S(1)}, u32[]{:S(2)}, u32[]{:S(2)}) async-start(bf16[8,128,128]{2,1,0:T(8,128)(2,1)} %bitcast.43), calls=%async_computation.4 | async-start | bytes 524288 | tf_op jit(solution)/shard_map/all_to_all | solution.py:29
  130.1 12.9 %collective-permute-start.5 = (bf16[1024,128]{1,0:T(8,128)(2,1)}, bf16[1024,128]{1,0:T(8,128)(2,1)S(1)}, u32[]{:S(2)}, u32[]{:S(2)}) collective-permute-start(bf16[1024,128]{1,0:T(8,128)(2,1)} %project.3), channel_id=1, source_target_pairs={{0,64},{64,0},{1,65},{65,1},{2,66},{66,2},{3,67},{67,3},{4,68},{68... | collective-permute-start | bytes 786440 | tf_op jit(solution)/shard_map/ppermute | solution.py:203
  132.7 10.3 %copy-start.6 = (bf16[1024,128]{1,0:T(8,128)(2,1)S(1)}, bf16[1024,128]{1,0:T(8,128)(2,1)}, u32[]{:S(2)}) copy-start(bf16[1024,128]{1,0:T(8,128)(2,1)} %project.3) | copy-start | bytes 786436
  133.6 67.6 %collective-permute-start.4 = (bf16[1024,128]{1,0:T(8,128)(2,1)S(1)}, bf16[1024,128]{1,0:T(8,128)(2,1)S(1)}, u32[]{:S(2)}, u32[]{:S(2)}) collective-permute-start(bf16[1024,128]{1,0:T(8,128)(2,1)S(1)} %copy-done.7), channel_id=1, source_target_pairs={{0,512},{1,513},{2,514},{3,515},{4,516},{5,517},{6,518},{7,519},{8... | collective-permute-start | bytes 786440 | tf_op jit(solution)/shard_map/ppermute | solution.py:235
  137.7 13.7 %all-to-all-start.3 = ((bf16[8,128,256]{2,1,0:T(8,128)(2,1)}), bf16[8,128,256]{2,1,0:T(8,128)(2,1)S(1)}, u32[]{:S(2)}, u32[]{:S(2)}) async-start(bf16[8,128,256]{2,1,0:T(8,128)(2,1)} %bitcast.30), calls=%async_computation.3 | async-start | bytes 1048576 | tf_op jit(solution)/shard_map/all_to_all | solution.py:29
  151.4 0.8 copy-start.5
  201.2 3.4 %copy-start.10 = (bf16[1024,128]{1,0:T(8,128)(2,1)}, bf16[1024,128]{1,0:T(8,128)(2,1)S(1)}, u32[]{:S(2)}) copy-start(bf16[1024,128]{1,0:T(8,128)(2,1)S(1)} %collective-permute-done.4.a_ref) | copy-start | bytes 786436
  201.2 3.4 %collective-permute-start.6 = (bf16[1024,128]{1,0:T(8,128)(2,1)S(1)}, bf16[1024,128]{1,0:T(8,128)(2,1)S(1)}, u32[]{:S(2)}, u32[]{:S(2)}) collective-permute-start(bf16[1024,128]{1,0:T(8,128)(2,1)S(1)} %collective-permute-done.4.a_ref), channel_id=1, source_target_pairs={{0,64},{64,0},{1,65},{65,1},{2,66},{66,2},{3,67},{67,3},{4,68},{68... | collective-permute-start | bytes 786440 | tf_op jit(solution)/shard_map/ppermute | solution.py:203
  204.6 0.7 copy-start.11

commit v5 on v4

--- a/solution.py
+++ b/solution.py
@@ -141,7 +141,7 @@
     )(q, k, v)
 
 
-def attend_more(who, q, first, partner, acc, st):
+def attend_more(h, who, q, first, partner, acc, st):
     part = 512
 
     def kernel(w_ref, q_ref, a_ref, b_ref, acc_ref, st_ref, o_ref, kv):
@@ -152,48 +152,45 @@
 
         @pl.when(w_ref[0] == 0)
         def _():
-            for h in range(2):
-                col = pl.ds(h * HEAD, HEAD)
-                o_ref[:, col] = (acc_ref[:, col] / st_ref[:, 2 + h : 3 + h]).astype(jnp.bfloat16)
+            o_ref[...] = (acc_ref[...] / st_ref[:, 2 + h : 3 + h]).astype(jnp.bfloat16)
 
         @pl.when(w_ref[0] != 0)
         def _():
-            for h in range(2):
-                col = pl.ds(h * HEAD, HEAD)
-                tiles = [
-                    lax.dot_general(
-                        q_ref[:, col],
-                        kv[0, t : t + part],
-                        NT,
-                        preferred_element_type=jnp.float32,
-                    )
-                    for t in range(0, 1024, part)
-                ]
-                m0 = st_ref[:, h : h + 1]
-                m1 = m0
-                for s in tiles:
-                    m1 = jnp.maximum(m1, jnp.max(s, axis=1, keepdims=True))
-                fade = jnp.exp2((m0 - m1) * SCALE2)
-                total = st_ref[:, 2 + h : 3 + h] * fade
-                out = acc_ref[:, col] * fade
-                for t, s in enumerate(tiles):
-                    p = jnp.exp2((s - m1) * SCALE2)
-                    total = total + jnp.sum(p, axis=1, keepdims=True)
-                    out = out + jnp.dot(
-                        p.astype(jnp.bfloat16),
-                        kv[1, t * part : (t + 1) * part],
-                        preferred_element_type=jnp.float32,
-                    )
-                o_ref[:, col] = (out / total).astype(jnp.bfloat16)
-
+            tiles = [
+                lax.dot_general(
+                    q_ref[...],
+                    kv[0, t : t + part],
+                    NT,
+                    preferred_element_type=jnp.float32,
+                )
+                for t in range(0, 1024, part)
+            ]
+            m0 = st_ref[:, h : h + 1]
+            m1 = m0
+            for s in tiles:
+                m1 = jnp.maximum(m1, jnp.max(s, axis=1, keepdims=True))
+            fade = jnp.exp2((m0 - m1) * SCALE2)
+            total = st_ref[:, 2 + h : 3 + h] * fade
+            out = acc_ref[...] * fade
+            for t, s in enumerate(tiles):
+                p = jnp.exp2((s - m1) * SCALE2)
+                total = total + jnp.sum(p, axis=1, keepdims=True)
+                out = out + jnp.dot(
+                    p.astype(jnp.bfloat16),
+                    kv[1, t * part : (t + 1) * part],
+                    preferred_element_type=jnp.float32,
+                )
+            o_ref[...] = (out / total).astype(jnp.bfloat16)
+
+    head = pl.BlockSpec((QB, HEAD), lambda i: (i, h))
     row = lambda width: pl.BlockSpec((QB, width), lambda i: (i, 0))
     whole = pl.BlockSpec((1024, HEAD), lambda i: (0, 0))
     return pl.pallas_call(
         kernel,
         grid=(1024 // QB,),
-        out_shape=jax.ShapeDtypeStruct((1024, 256), jnp.bfloat16),
-        in_specs=[SM, row(256), whole, whole, row(256), row(4)],
-        out_specs=row(256),
+        out_shape=jax.ShapeDtypeStruct((1024, HEAD), jnp.bfloat16),
+        in_specs=[SM, head, whole, whole, head, row(4)],
+        out_specs=row(HEAD),
         scratch_shapes=[pltpu.VMEM((2, 1024, HEAD), jnp.bfloat16)],
         name="attend_more",
     )(who, q, first, partner, acc, st)
@@ -248,8 +245,11 @@
         (first, state, cache_keys, cache_values)
     )
     partner = swap_cores(first)
-    state = attend_more(jnp.stack([zh, c]), q, first, partner, *state)
-    out = exchange(state.reshape(8, 128, 256), ("x", "c"))
+    outs = []
+    for h in range(2):
+        out = attend_more(h, jnp.stack([zh, c]), q, first, partner, *state)
+        outs.append(exchange(out.reshape(8, 128, HEAD), ("x", "c")))
+    out = jnp.concatenate(outs, axis=1).reshape(16, 128, HEAD)
     attended = out.transpose(1, 0, 2).reshape(1, 128, 2048)
     return cache_keys, cache_values, attended
 

time: 231 us -> 236 us (1.022)
  starting transfers between devices: 41.2 us -> 46 us
  blocking collectives: 58.2 us -> 53.9 us
  Pallas kernels: 24.3 us -> 27.4 us
    all_to_all x4 -> x5, starting transfers between devices: 24.2 us -> 29 us  [exchange(): return lax.all_to_all(x, axes, 0, 0, tiled=True)]
    all_to_all x2, blocking collectives: 58.2 us -> 53.9 us  [exchange(): return lax.all_to_all(x, axes, 0, 0, tiled=True)]
    pallas_call x1 -> x2, Pallas kernels: 7.79 us -> 10.9 us  [attend_more(): pl.pallas_call(kernel, grid=(1024 // QB,), out_shape=jax.ShapeDtypeStruct...]
    all_to_all x4 -> x5, waiting for transfers between devices: 19.1 us -> 21.1 us  [exchange(): return lax.all_to_all(x, axes, 0, 0, tiled=True)]
  transfers between devices with their start and end apart: 11 -> 12, of which waited for: 8 -> 9; matrix products, arithmetic and copies ran while one was open for 5% -> 5% of each run, Pallas kernels for 2% -> 5%
where the time goes in v5:
time: 236 us; the launch traced here: 235 us
  waiting for transfers between devices  89.2 us (38%)
  blocking collectives  53.9 us (23%)
  starting transfers between devices  46 us (19%)
  Pallas kernels  27.4 us (12%)
  other arithmetic  9.82 us (4%)
  local copies, waits for them, and re-layouts  7.93 us (3%)
    all_to_all x2, blocking collectives, exchange(): return lax.all_to_all(x, axes, 0, 0, tiled=True)  53.9 us
    ppermute x1, waiting for transfers between devices, layer(): first = lax.ppermute(sent, RING, [(i, i + 16) for i in range(16)])  43.4 us
    all_to_all x5, starting transfers between devices, exchange(): return lax.all_to_all(x, axes, 0, 0, tiled=True)  29 us
    all_to_all x5, waiting for transfers between devices, exchange(): return lax.all_to_all(x, axes, 0, 0, tiled=True)  21.1 us
    ppermute x3, waiting for transfers between devices, layer(): rows.append(lax.ppermute(n, 'x', [(i, (i + s) % 4) for i in range(4)]))  20.2 us
    pallas_call x2, Pallas kernels, attend_more(): pl.pallas_call(kernel, grid=(1024 // QB,), out_shape=jax.ShapeDtypeStruct...  10.9 us
    ppermute x3, starting transfers between devices, layer(): rows.append(lax.ppermute(n, 'x', [(i, (i + s) % 4) for i in range(4)]))  9.55 us
    pallas_call x2, Pallas kernels, project(): pl.pallas_call(kernel, out_shape=jax.ShapeDtypeStruct((1024, HEAD), jnp.b...  7.49 us
  transfers between devices with their start and end apart: 12, of which 9 were waited for; matrix products, arithmetic and copies ran while one was open for 5% of the time, Pallas kernels for 5%

profile of v5, /device:TPU:968, one launch (start us, length us, event | category | flops | bytes accessed | tf_op | source)
XLA Modules:
  0.0 235.2 jit_solution(14540786771434639225)
XLA Ops:
  2.4 11.0 %all-to-all-start = ((bf16[128,8,128]{2,1,0:T(8,128)(2,1)}), bf16[128,8,128]{2,1,0:T(8,128)(2,1)S(1)}, u32[]{:S(2)}, u32[]{:S(2)}) async-start(bf16[128,8,128]{2,1,0:T(8,128)(2,1)} %bitcast.4), calls=%async_computation | async-start | bytes 524288 | tf_op jit(solution)/shard_map/all_to_all | solution.py:29
  15.3 8.7 %all-to-all-done.x_ref = bf16[128,8,128]{2,1,0:T(8,128)(2,1)S(1)} async-done(((bf16[128,8,128]{2,1,0:T(8,128)(2,1)}), bf16[128,8,128]{2,1,0:T(8,128)(2,1)S(1)}, u32[]{:S(2)}, u32[]{:S(2)}) %all-to-all-start) | async-done | bytes 262176 | tf_op jit(solution)/shard_map/all_to_all | solution.py:29
  26.3 43.1 %all_to_all.35 = bf16[8,8,8,128]{3,2,1,0:T(8,128)(2,1)} all-to-all(bf16[8,8,8,128]{3,2,1,0:T(8,128)(2,1)} %pick.2), channel_id=1, replica_groups=mesh['zh'=2,'x'=4,'c'=2,'y'=4,'zf'=4,'zn'=4] {'zh','zf'}, dimensions={0} | all-to-all | bytes 262144 | tf_op jit(solution)/shard_map/all_to_all | solution.py:29
  71.2 5.5 %all-to-all-start.2 = ((bf16[16,16,8,128]{3,2,1,0:T(8,128)(2,1)}), bf16[16,16,8,128]{3,2,1,0:T(8,128)(2,1)S(1)}, u32[]{:S(2)}, u32[]{:S(2)}) async-start(bf16[16,16,8,128]{3,2,1,0:T(8,128)(2,1)} %pick.3), calls=%async_computation.2 | async-start | bytes 1048576 | tf_op jit(solution)/shard_map/all_to_all | solution.py:29
  76.7 2.5 %collective-permute-start = (bf16[128,2048]{1,0:T(8,128)(2,1)S(1)}, bf16[128,2048]{1,0:T(8,128)(2,1)S(1)}, u32[]{:S(2)}, u32[]{:S(2)}) collective-permute-start(bf16[128,2048]{1,0:T(8,128)(2,1)S(1)} %bitcast.44), channel_id=1, source_target_pairs={{0,128},{128,256},{256,384},{384,0},{1,129},{129,257},{257,385},{3... | collective-permute-start | bytes 1572872 | tf_op jit(solution)/shard_map/ppermute | solution.py:215
  79.2 3.5 %collective-permute-start.1 = (bf16[128,2048]{1,0:T(8,128)(2,1)S(1)}, bf16[128,2048]{1,0:T(8,128)(2,1)S(1)}, u32[]{:S(2)}, u32[]{:S(2)}) collective-permute-start(bf16[128,2048]{1,0:T(8,128)(2,1)S(1)} %bitcast.45), channel_id=1, source_target_pairs={{0,256},{128,384},{256,0},{384,128},{1,257},{129,385},{257,1},{385... | collective-permute-start | bytes 1572872 | tf_op jit(solution)/shard_map/ppermute | solution.py:215
  82.7 3.5 %collective-permute-start.2 = (bf16[128,2048]{1,0:T(8,128)(2,1)S(1)}, bf16[128,2048]{1,0:T(8,128)(2,1)S(1)}, u32[]{:S(2)}, u32[]{:S(2)}) collective-permute-start(bf16[128,2048]{1,0:T(8,128)(2,1)S(1)} %bitcast.46), channel_id=1, source_target_pairs={{0,384},{128,0},{256,128},{384,256},{1,385},{129,1},{257,129},{385... | collective-permute-start | bytes 1572872 | tf_op jit(solution)/shard_map/ppermute | solution.py:215
  86.2 17.7 %collective-permute-done.a1 = bf16[128,2048]{1,0:T(8,128)(2,1)S(1)} collective-permute-done((bf16[128,2048]{1,0:T(8,128)(2,1)S(1)}, bf16[128,2048]{1,0:T(8,128)(2,1)S(1)}, u32[]{:S(2)}, u32[]{:S(2)}) %collective-permute-start) | collective-permute-done | bytes 524320 | tf_op jit(solution)/shard_map/ppermute | solution.py:215
  104.0 2.5 %collective-permute-done.2.a3 = bf16[128,2048]{1,0:T(8,128)(2,1)S(1)} collective-permute-done((bf16[128,2048]{1,0:T(8,128)(2,1)S(1)}, bf16[128,2048]{1,0:T(8,128)(2,1)S(1)}, u32[]{:S(2)}, u32[]{:S(2)}) %collective-permute-start.2) | collective-permute-done | bytes 524320 | tf_op jit(solution)/shard_map/ppermute | solution.py:215
  110.6 3.7 %collective-permute-done.3.b_ref = bf16[512,2048]{1,0:T(8,128)(2,1)S(1)} collective-permute-done((bf16[512,2048]{1,0:T(8,128)(2,1)}, bf16[512,2048]{1,0:T(8,128)(2,1)S(1)}, u32[]{:S(2)}, u32[]{:S(2)}) %collective-permute-start.3) | collective-permute-done | bytes 2097184 | tf_op jit(solution)/shard_map/ppermute | solution.py:200
  120.0 6.0 %project.3 = bf16[1024,128]{1,0:T(8,128)(2,1)} custom-call(s32[9]{0:T(128)} %get-tuple-element.28.p_ref, bf16[128,2048]{1,0:T(8,128)(2,1)} %bitcast.43, bf16[128,2048]{1,0:T(8,128)(2,1)} %copy-done.3, bf16[128,2048]{1,0:T(8,128)(2,1)} %copy-done.4, bf16[128,2048]{1,0:T(8,128)(2,1)} %copy-done.5, bf16[512,2048]{1,0:T(8,128)(2,1)} %copy-done, ...), custom_call_target="tpu_custom_call" | custom-call | tf_op jit(solution)/shard_map/project/pallas_call | solution.py:96
  126.0 4.0 %all-to-all-start.4 = ((bf16[8,128,128]{2,1,0:T(8,128)(2,1)}), bf16[8,128,128]{2,1,0:T(8,128)(2,1)S(1)}, u32[]{:S(2)}, u32[]{:S(2)}) async-start(bf16[8,128,128]{2,1,0:T(8,128)(2,1)} %bitcast.48), calls=%async_computation.4 | async-start | bytes 524288 | tf_op jit(solution)/shard_map/all_to_all | solution.py:29
  130.1 2.4 %collective-permute-start.5 = (bf16[1024,128]{1,0:T(8,128)(2,1)}, bf16[1024,128]{1,0:T(8,128)(2,1)S(1)}, u32[]{:S(2)}, u32[]{:S(2)}) collective-permute-start(bf16[1024,128]{1,0:T(8,128)(2,1)} %project.3), channel_id=1, source_target_pairs={{0,64},{64,0},{1,65},{65,1},{2,66},{66,2},{3,67},{67,3},{4,68},{68... | collective-permute-start | bytes 786440 | tf_op jit(solution)/shard_map/ppermute | solution.py:200
  134.8 2.8 %all-to-all-done.4 = bf16[8,128,128]{2,1,0:T(8,128)(2,1)S(1)} async-done(((bf16[8,128,128]{2,1,0:T(8,128)(2,1)}), bf16[8,128,128]{2,1,0:T(8,128)(2,1)S(1)}, u32[]{:S(2)}, u32[]{:S(2)}) %all-to-all-start.4) | async-done | bytes 262176 | tf_op jit(solution)/shard_map/all_to_all | solution.py:29
  137.6 3.7 %all-to-all-start.3 = ((bf16[8,128,256]{2,1,0:T(8,128)(2,1)}), bf16[8,128,256]{2,1,0:T(8,128)(2,1)S(1)}, u32[]{:S(2)}, u32[]{:S(2)}) async-start(bf16[8,128,256]{2,1,0:T(8,128)(2,1)} %bitcast.34), calls=%async_computation.3 | async-start | bytes 1048576 | tf_op jit(solution)/shard_map/all_to_all | solution.py:29
  143.8 7.5 %all-to-all-done.3 = bf16[8,128,256]{2,1,0:T(8,128)(2,1)S(1)} async-done(((bf16[8,128,256]{2,1,0:T(8,128)(2,1)}), bf16[8,128,256]{2,1,0:T(8,128)(2,1)S(1)}, u32[]{:S(2)}, u32[]{:S(2)}) %all-to-all-start.3) | async-done | bytes 524320 | tf_op jit(solution)/shard_map/all_to_all | solution.py:29
  152.1 5.6 %attend_own.1 = (f32[1024,256]{1,0:T(8,128)}, f32[1024,4]{1,0:T(8,128)}) custom-call(bf16[1024,256]{1,0:T(8,128)(2,1)} %bitcast.37, bf16[1024,128]{1,0:T(8,128)(2,1)} %get-tuple-element.22.k_ref, bf16[1024,128]{1,0:T(8,128)(2,1)} %get-tuple-element.21.v_ref), custom_call_target="tpu_custom_call" | custom-call | tf_op jit(solution)/shard_map/attend_own/pallas_call | solution.py:135
  157.7 43.4 %collective-permute-done.4.a_ref = bf16[1024,128]{1,0:T(8,128)(2,1)S(1)} collective-permute-done((bf16[1024,128]{1,0:T(8,128)(2,1)S(1)}, bf16[1024,128]{1,0:T(8,128)(2,1)S(1)}, u32[]{:S(2)}, u32[]{:S(2)}) %collective-permute-start.4) | collective-permute-done | bytes 262176 | tf_op jit(solution)/shard_map/ppermute | solution.py:232
  201.1 1.9 collective-permute-start.6
  205.2 5.5 %attend_more.2 = bf16[1024,128]{1,0:T(8,128)(2,1)} custom-call(s32[2]{0:T(128)} %pad_add_fusion.3.w_ref, bf16[1024,256]{1,0:T(8,128)(2,1)} %bitcast.38, bf16[1024,128]{1,0:T(8,128)(2,1)} %copy-done.8, bf16[1024,128]{1,0:T(8,128)(2,1)} %copy-done.9, f32[1024,256]{1,0:T(8,128)} %get-tuple-element.19.acc_ref, f32[1024,4]{1,0:T(8,128)} %get-tuple-element.20.st_ref), custom_call_target="tpu_custom_call" | custom-call | tf_op jit(solution)/shard_map/attend_more/pallas_call | solution.py:188
  210.7 4.8 %all-to-all-start.5 = ((bf16[8,128,128]{2,1,0:T(8,128)(2,1)}), bf16[8,128,128]{2,1,0:T(8,128)(2,1)S(1)}, u32[]{:S(2)}, u32[]{:S(2)}) async-start(bf16[8,128,128]{2,1,0:T(8,128)(2,1)} %bitcast.53), calls=%async_computation.5 | async-start | bytes 524288 | tf_op jit(solution)/shard_map/all_to_all | solution.py:29
  215.5 5.5 %attend_more.3 = bf16[1024,128]{1,0:T(8,128)(2,1)} custom-call(s32[2]{0:T(128)} %pad_add_fusion.3.w_ref, bf16[1024,256]{1,0:T(8,128)(2,1)} %bitcast.39, bf16[1024,128]{1,0:T(8,128)(2,1)} %copy-done.8, bf16[1024,128]{1,0:T(8,128)(2,1)} %copy-done.9, f32[1024,256]{1,0:T(8,128)} %get-tuple-element.19.acc_ref, f32[1024,4]{1,0:T(8,128)} %get-tuple-element.20.st_ref), custom_call_target="tpu_custom_call" | custom-call | tf_op jit(solution)/shard_map/attend_more/pallas_call | solution.py:188
  220.9 2.0 all-to-all-done.5
  223.0 10.8 %all_to_all.36 = bf16[8,128,128]{2,1,0:T(8,128)(2,1)S(1)} all-to-all(bf16[8,128,128]{2,1,0:T(8,128)(2,1)} %bitcast.54), channel_id=1, replica_groups=mesh['zh'=2,'x'=4,'c'=2,'y'=4,'zf'=4,'zn'=4] {'x','c'}, dimensions={0} | all-to-all | bytes 524288 | tf_op jit(solution)/shard_map/all_to_all | solution.py:29
  (57 shorter events, 26.7 us)
Async XLA Ops:
  0.6 76.0 %copy-start.2 = (bf16[1,128,2048]{2,1,0:T(8,128)(2,1)S(1)}, bf16[1,128,2048]{2,1,0:T(8,128)(2,1)}, u32[]{:S(2)}) copy-start(bf16[1,128,2048]{2,1,0:T(8,128)(2,1)} %param.6) | copy-start | bytes 1572868
  2.4 21.5 %all-to-all-start = ((bf16[128,8,128]{2,1,0:T(8,128)(2,1)}), bf16[128,8,128]{2,1,0:T(8,128)(2,1)S(1)}, u32[]{:S(2)}, u32[]{:S(2)}) async-start(bf16[128,8,128]{2,1,0:T(8,128)(2,1)} %bitcast.4), calls=%async_computation | async-start | bytes 524288 | tf_op jit(solution)/shard_map/all_to_all | solution.py:29
  24.0 0.7 copy-start.10
  71.2 46.4 %all-to-all-start.2 = ((bf16[16,16,8,128]{3,2,1,0:T(8,128)(2,1)}), bf16[16,16,8,128]{3,2,1,0:T(8,128)(2,1)S(1)}, u32[]{:S(2)}, u32[]{:S(2)}) async-start(bf16[16,16,8,128]{3,2,1,0:T(8,128)(2,1)} %pick.3), calls=%async_computation.2 | async-start | bytes 1048576 | tf_op jit(solution)/shard_map/all_to_all | solution.py:29
  76.7 27.3 %collective-permute-start = (bf16[128,2048]{1,0:T(8,128)(2,1)S(1)}, bf16[128,2048]{1,0:T(8,128)(2,1)S(1)}, u32[]{:S(2)}, u32[]{:S(2)}) collective-permute-start(bf16[128,2048]{1,0:T(8,128)(2,1)S(1)} %bitcast.44), channel_id=1, source_target_pairs={{0,128},{128,256},{256,384},{384,0},{1,129},{129,257},{257,385},{3... | collective-permute-start | bytes 1572872 | tf_op jit(solution)/shard_map/ppermute | solution.py:215
  79.2 24.8 %collective-permute-start.1 = (bf16[128,2048]{1,0:T(8,128)(2,1)S(1)}, bf16[128,2048]{1,0:T(8,128)(2,1)S(1)}, u32[]{:S(2)}, u32[]{:S(2)}) collective-permute-start(bf16[128,2048]{1,0:T(8,128)(2,1)S(1)} %bitcast.45), channel_id=1, source_target_pairs={{0,256},{128,384},{256,0},{384,128},{1,257},{129,385},{257,1},{385... | collective-permute-start | bytes 1572872 | tf_op jit(solution)/shard_map/ppermute | solution.py:215
  82.7 23.7 %collective-permute-start.2 = (bf16[128,2048]{1,0:T(8,128)(2,1)S(1)}, bf16[128,2048]{1,0:T(8,128)(2,1)S(1)}, u32[]{:S(2)}, u32[]{:S(2)}) collective-permute-start(bf16[128,2048]{1,0:T(8,128)(2,1)S(1)} %bitcast.46), channel_id=1, source_target_pairs={{0,384},{128,0},{256,128},{384,256},{1,385},{129,1},{257,129},{385... | collective-permute-start | bytes 1572872 | tf_op jit(solution)/shard_map/ppermute | solution.py:215
  103.9 4.1 %copy-start.3 = (bf16[128,2048]{1,0:T(8,128)(2,1)}, bf16[128,2048]{1,0:T(8,128)(2,1)S(1)}, u32[]{:S(2)}) copy-start(bf16[128,2048]{1,0:T(8,128)(2,1)S(1)} %collective-permute-done.a1) | copy-start | bytes 1572868
  104.0 4.1 %copy-start.4 = (bf16[128,2048]{1,0:T(8,128)(2,1)}, bf16[128,2048]{1,0:T(8,128)(2,1)S(1)}, u32[]{:S(2)}) copy-start(bf16[128,2048]{1,0:T(8,128)(2,1)S(1)} %collective-permute-done.1.a2) | copy-start | bytes 1572868
  106.5 1.6 copy-start.5
  108.1 6.3 %collective-permute-start.3 = (bf16[512,2048]{1,0:T(8,128)(2,1)}, bf16[512,2048]{1,0:T(8,128)(2,1)S(1)}, u32[]{:S(2)}, u32[]{:S(2)}) collective-permute-start(bf16[512,2048]{1,0:T(8,128)(2,1)} %pad_maximum_fusion), channel_id=1, source_target_pairs={{0,64},{64,0},{1,65},{65,1},{2,66},{66,2},{3,67},{67,3},{4,68},{68... | collective-permute-start | bytes 6291464 | tf_op jit(solution)/shard_map/ppermute | solution.py:200
  114.3 3.2 %copy-start = (bf16[512,2048]{1,0:T(8,128)(2,1)}, bf16[512,2048]{1,0:T(8,128)(2,1)S(1)}, u32[]{:S(2)}) copy-start(bf16[512,2048]{1,0:T(8,128)(2,1)S(1)} %collective-permute-done.3.b_ref) | copy-start | bytes 6291460
  120.0 12.5 %copy-start.11 = (bf16[1,128,2048]{2,1,0:T(8,128)(2,1)S(1)}, bf16[1,128,2048]{2,1,0:T(8,128)(2,1)}, u32[]{:S(2)}) copy-start(bf16[1,128,2048]{2,1,0:T(8,128)(2,1)} %param.5) | copy-start | bytes 1572868
  126.0 7.5 %copy-start.7 = (bf16[1024,128]{1,0:T(8,128)(2,1)S(1)}, bf16[1024,128]{1,0:T(8,128)(2,1)}, u32[]{:S(2)}) copy-start(bf16[1024,128]{1,0:T(8,128)(2,1)} %project.2.rest_0_) | copy-start | bytes 786436
  126.0 11.6 %all-to-all-start.4 = ((bf16[8,128,128]{2,1,0:T(8,128)(2,1)}), bf16[8,128,128]{2,1,0:T(8,128)(2,1)S(1)}, u32[]{:S(2)}, u32[]{:S(2)}) async-start(bf16[8,128,128]{2,1,0:T(8,128)(2,1)} %bitcast.48), calls=%async_computation.4 | async-start | bytes 524288 | tf_op jit(solution)/shard_map/all_to_all | solution.py:29
  130.1 12.9 %collective-permute-start.5 = (bf16[1024,128]{1,0:T(8,128)(2,1)}, bf16[1024,128]{1,0:T(8,128)(2,1)S(1)}, u32[]{:S(2)}, u32[]{:S(2)}) collective-permute-start(bf16[1024,128]{1,0:T(8,128)(2,1)} %project.3), channel_id=1, source_target_pairs={{0,64},{64,0},{1,65},{65,1},{2,66},{66,2},{3,67},{67,3},{4,68},{68... | collective-permute-start | bytes 786440 | tf_op jit(solution)/shard_map/ppermute | solution.py:200
  132.6 10.3 %copy-start.6 = (bf16[1024,128]{1,0:T(8,128)(2,1)S(1)}, bf16[1024,128]{1,0:T(8,128)(2,1)}, u32[]{:S(2)}) copy-start(bf16[1024,128]{1,0:T(8,128)(2,1)} %project.3) | copy-start | bytes 786436
  133.5 67.6 %collective-permute-start.4 = (bf16[1024,128]{1,0:T(8,128)(2,1)S(1)}, bf16[1024,128]{1,0:T(8,128)(2,1)S(1)}, u32[]{:S(2)}, u32[]{:S(2)}) collective-permute-start(bf16[1024,128]{1,0:T(8,128)(2,1)S(1)} %copy-done.7), channel_id=1, source_target_pairs={{0,512},{1,513},{2,514},{3,515},{4,516},{5,517},{6,518},{7,519},{8... | collective-permute-start | bytes 786440 | tf_op jit(solution)/shard_map/ppermute | solution.py:232
  137.6 13.7 %all-to-all-start.3 = ((bf16[8,128,256]{2,1,0:T(8,128)(2,1)}), bf16[8,128,256]{2,1,0:T(8,128)(2,1)S(1)}, u32[]{:S(2)}, u32[]{:S(2)}) async-start(bf16[8,128,256]{2,1,0:T(8,128)(2,1)} %bitcast.34), calls=%async_computation.3 | async-start | bytes 1048576 | tf_op jit(solution)/shard_map/all_to_all | solution.py:29
  151.3 0.8 copy-start.1
  201.1 3.4 %copy-start.8 = (bf16[1024,128]{1,0:T(8,128)(2,1)}, bf16[1024,128]{1,0:T(8,128)(2,1)S(1)}, u32[]{:S(2)}) copy-start(bf16[1024,128]{1,0:T(8,128)(2,1)S(1)} %collective-permute-done.4.a_ref) | copy-start | bytes 786436
  201.1 3.4 %collective-permute-start.6 = (bf16[1024,128]{1,0:T(8,128)(2,1)S(1)}, bf16[1024,128]{1,0:T(8,128)(2,1)S(1)}, u32[]{:S(2)}, u32[]{:S(2)}) collective-permute-start(bf16[1024,128]{1,0:T(8,128)(2,1)S(1)} %collective-permute-done.4.a_ref), channel_id=1, source_target_pairs={{0,64},{64,0},{1,65},{65,1},{2,66},{66,2},{3,67},{67,3},{4,68},{68... | collective-permute-start | bytes 786440 | tf_op jit(solution)/shard_map/ppermute | solution.py:200
  204.5 0.7 copy-start.9
  210.7 12.3 %all-to-all-start.5 = ((bf16[8,128,128]{2,1,0:T(8,128)(2,1)}), bf16[8,128,128]{2,1,0:T(8,128)(2,1)S(1)}, u32[]{:S(2)}, u32[]{:S(2)}) async-start(bf16[8,128,128]{2,1,0:T(8,128)(2,1)} %bitcast.53), calls=%async_computation.5 | async-start | bytes 524288 | tf_op jit(solution)/shard_map/all_to_all | solution.py:29
